TPU v7x, 512 devices: a whole 4x8x8 slice. The times are simulated.
512 devices in a mesh: chan: 8 (over z), seq: 64 (over y, x, core).
Axes of the slice: x: 4, y: 8, z: 8, core: 2. Of those that a mesh axis runs over, the one named last changes fastest.
Arguments:
- inputs: bfloat16 [3, 8192, 2, 4096], P(None, 'seq', None, 'chan'), may hold values from -6 to 6
- decay_rate: float32 [4096], P('chan'), may hold values from 6.1035156e-05 to 0.03
- phase: float32 [4096], P('chan'), may hold values from -3.140625 to 3.140625
- keep: float32 [3, 8192], replicated, may hold values from 0.5 to 1
Outputs:
- states: bfloat16 [3, 8192, 2, 4096], P(None, 'seq', None, 'chan')
All inputs are finite; a program needn't handle non-finite values.
Results may differ from a plain program's by a relative error of at most 0.001.
Values sent between devices are 32-bit elements; how exact they have to be, the bound alone decides.
No kernel may reach another device: no remote copies, remote signals or barrier semaphores. Data moves between devices by JAX's collectives and lax.ppermute only.
A program may use at most 64 MiB of HBM per device.

v0:
```python
import jax
import jax.numpy as jnp
from jax import lax
from jax.sharding import Mesh
from jax.sharding import PartitionSpec as P

SEQ = ("seq_0", "seq_1", "seq_2")


def neutral_like(array, identity):
    return jax.tree.map(
        lambda part, zero: jnp.zeros_like(part) + jnp.asarray(zero, part.dtype), array, identity
    )


def gathered_once(array, axis):
    leaves = jax.tree.leaves(array)
    turns = sorted(range(len(leaves)), key=lambda k: -leaves[k].size)
    width = (1, *leaves[turns[0]].shape)[-1]
    lines = [
        jnp.pad(leaves[k].reshape(-1), (0, -leaves[k].size % width)).reshape(-1, width)
        for k in turns
    ]
    both, at, found = (lax.all_gather(jnp.concatenate(lines), axis), 0, {})
    for k, line in zip(turns, lines):
        slab = both[:, at : at + len(line)].reshape(len(both), -1)
        found[k] = slab[:, : leaves[k].size].reshape(-1, *leaves[k].shape)
        at += len(line)
    numbers = iter(range(len(leaves)))
    return jax.tree.map(lambda _: found[next(numbers)], array)


def prefix_by_axis(array, axes, combine, identity):
    before = start = neutral_like(array, identity)
    total = array
    for axis in reversed(axes):
        size, mine = (lax.axis_size(axis), lax.axis_index(axis))
        pieces = gathered_once(total, axis)
        inside, total = (start, start)
        for k in range(size):
            passed = k < mine
            total = combine(total, jax.tree.map(lambda part: part[k], pieces))
            inside = jax.tree.map(lambda new, old: jnp.where(passed, new, old), total, inside)
        before = combine(inside, before)
    return before


def compose(early, late):
    ear, eai, ebr, ebi = early
    lar, lai, lbr, lbi = late
    return (
        lar * ear - lai * eai,
        lar * eai + lai * ear,
        lar * ebr - lai * ebi + lbr,
        lar * ebi + lai * ebr + lbi,
    )


def reduce_block(items):
    count = items[0].shape[0]
    while count > 1 and count % 2 == 0:
        pairs = [part.reshape((count // 2, 2) + part.shape[1:]) for part in items]
        items = compose(tuple((p[:, 0] for p in pairs)), tuple((p[:, 1] for p in pairs)))
        count = count // 2
    result = tuple((part[0] for part in items))
    return result


def coefficients(decay_rate, phase):
    magnitude = jnp.exp(-decay_rate)
    gamma = jnp.sqrt(-jnp.expm1(-2.0 * decay_rate))
    return (magnitude * jnp.cos(phase), magnitude * jnp.sin(phase), gamma)


def shards(inputs, decay_rate, phase, keep):
    lam_re, lam_im, gamma = coefficients(decay_rate, phase)
    batch = inputs.shape[0]
    rows = inputs.shape[1]
    width = lam_re.shape[0]
    me = lax.axis_index(SEQ)
    offset = me * rows
    factors = jnp.transpose(lax.dynamic_slice_in_dim(keep, offset, rows, 1))
    dec_re = factors[:, :, None] * lam_re[None, None, :]
    dec_im = factors[:, :, None] * lam_im[None, None, :]
    leading = jnp.transpose(inputs, (1, 2, 0, 3))
    drive_re = leading[:, 0].astype(jnp.float32) * gamma[None, None, :]
    drive_im = leading[:, 1].astype(jnp.float32) * gamma[None, None, :]
    items = (dec_re, dec_im, drive_re, drive_im)
    zeros = jnp.zeros((batch, width), jnp.float32)
    identity = (jnp.ones((batch, width), jnp.float32), zeros, zeros, zeros)
    totals = reduce_block(items)
    incoming = prefix_by_axis(totals, SEQ, compose, identity)
    carry_re = incoming[2]
    carry_im = incoming[3]
    first_re = drive_re[0] + dec_re[0] * carry_re - dec_im[0] * carry_im
    first_im = drive_im[0] + dec_re[0] * carry_im + dec_im[0] * carry_re
    drive_re = drive_re.at[0].set(first_re)
    drive_im = drive_im.at[0].set(first_im)
    _, _, final_re, final_im = lax.associative_scan(
        compose, (dec_re, dec_im, drive_re, drive_im), axis=0
    )
    joined = jnp.stack([final_re, final_im], axis=1)
    return jnp.transpose(joined, (2, 0, 1, 3)).astype(jnp.bfloat16)


def solution(mesh):
    split = Mesh(
        mesh.devices.reshape(mesh.shape["chan"], 8, 4, 2), ("chan", "seq_0", "seq_1", "seq_2")
    )
    in_specs = (P(None, SEQ, None, "chan"), P("chan"), P("chan"), P())
    out_specs = P(None, SEQ, None, "chan")
    return jax.shard_map(
        shards, mesh=split, in_specs=in_specs, out_specs=out_specs, check_vma=False
    )
```

profile of v0, /device:TPU:4, one launch (start us, length us, event | category | flops | bytes accessed | tf_op | source)
XLA Modules:
  0.0 91.0 jit_solution(13193955783929035716)
XLA Ops:
  0.0 0.9 copy-done
  0.9 0.7 copy-done.9
  1.6 0.1 mul.1152
  1.9 1.2 %copy.664 = bf16[3,128,2,512]{3,1,0,2:T(8,128)(2,1)S(1)} copy(bf16[3,128,2,512]{3,2,1,0:T(2,128)(2,1)} %param.8) | data formatting | bytes 1572864 | tf_op args[0]
  3.1 0.2 slice_convert_fusion.1
  3.3 0.5 reshape.551
  3.8 0.5 reshape.552
  4.3 0.4 copy_multiply_fusion.1
  4.7 0.4 multiply_subtract_fusion.1
  5.1 0.2 sub.311
  5.3 0.2 add.809
  5.6 0.2 add.826
  5.8 0.2 add.823
  6.0 2.9 %fusion.2 = (f32[32,3,512]{2,0,1:T(8,128)S(1)}, f32[32,3,512]{2,0,1:T(8,128)S(1)}, f32[32,3,512]{2,0,1:T(8,128)S(1)}, f32[32,3,512]{2,0,1:T(8,128)S(1)}) fusion(f32[32,2,3,512]{3,1,0,2:T(2,128)S(1)} %add.826, f32[32,2,3,512]{3,1,0,2:T(2,128)S(1)} %add.823, f32[32,2,3,512]{3,1,0,2:T(2,128)S(1)} %add.809, f32[32,2,3,512]{3,1,0,2:T(2,128)S(1)} %sub.311), kind=kLoop, calls=%fused_computation.33 | loop fusion | flops 688128 | bytes 2359296 | tf_op jit(solution)/shard_map/add | solution.py:55
  9.4 1.4 %fusion.4 = (f32[16,3,512]{2,0,1:T(8,128)S(1)}, f32[16,3,512]{2,0,1:T(8,128)S(1)}, f32[16,3,512]{2,0,1:T(8,128)S(1)}, f32[16,3,512]{2,0,1:T(8,128)S(1)}) fusion(f32[16,2,3,512]{3,1,0,2:T(2,128)S(1)} %add.831, f32[16,2,3,512]{3,1,0,2:T(2,128)S(1)} %add.828, f32[16,2,3,512]{3,1,0,2:T(2,128)S(1)} %add.811, f32[16,2,3,512]{3,1,0,2:T(2,128)S(1)} %sub.313), kind=kLoop, calls=%fused_computation.49 | loop fusion | flops 344064 | bytes 1179648 | tf_op jit(solution)/shard_map/add | solution.py:55
  11.0 0.7 fusion.6
  11.9 0.4 fusion.8
  12.7 1.9 %all-gather.3 = f32[2,12,512]{2,1,0:T(8,128)S(1)} all-gather(f32[1,12,512]{2,1,0:T(8,128)S(1)} %maximum_bitcast_fusion.1), channel_id=2, replica_groups=mesh['chan'=8,'seq_0'=8,'seq_1'=4,'seq_2'=2] {'seq_2'}, dimensions={0}, use_global_device_ids=true | all-gather | bytes 73728 | tf_op jit(solution)/shard_map/all_gather | solution.py:24
  14.7 15.8 %all-gather.4 = f32[4,12,512]{2,1,0:T(8,128)S(1)} all-gather(f32[1,12,512]{2,1,0:T(8,128)S(1)} %maximum_bitcast_fusion.2), channel_id=3, replica_groups=mesh['chan'=8,'seq_0'=8,'seq_1'=4,'seq_2'=2] {'seq_1'}, dimensions={0}, use_global_device_ids=true | all-gather | bytes 122880 | tf_op jit(solution)/shard_map/all_gather | solution.py:24
  30.9 24.8 %all-gather.5 = f32[8,12,512]{2,1,0:T(8,128)S(1)} all-gather(f32[1,12,512]{2,1,0:T(8,128)S(1)} %maximum_bitcast_fusion.3), channel_id=4, replica_groups=mesh['chan'=8,'seq_0'=8,'seq_1'=4,'seq_2'=2] {'seq_0'}, dimensions={0}, use_global_device_ids=true | all-gather | bytes 221184 | tf_op jit(solution)/shard_map/all_gather | solution.py:24
  55.8 0.1 copy_add_fusion.6
  56.0 0.3 bitcast_multiply_fusion.1
  56.3 0.9 copy-done.1
  57.2 0.1 fusion.52
  57.3 1.4 %scatter.6 = f32[128,3,512]{2,0,1:T(8,128)} dynamic-update-slice(f32[128,3,512]{2,0,1:T(8,128)} %copy-done.1, f32[1,3,512]{2,0,1:T(1,128)S(1)} %get-tuple-element.48, s32[]{:T(128)} %constant.71.clone.1, s32[]{:T(128)} %constant.71.clone.1, s32[]{:T(128)} %constant.71.clone.1) | dynamic-update-slice | bytes 12292 | tf_op jit(solution)/shard_map/scatter | solution.py:97
  58.8 0.3 scatter.9
  59.0 1.6 %slice.995 = f32[63,3,512]{2,0,1:T(8,128)} slice(f32[128,3,512]{2,0,1:T(8,128)S(1)} %scatter.9), slice={[2:128:2], [0:3:1], [0:512:1]} | slice | bytes 774144 | tf_op jit(solution)/shard_map/slice | solution.py:99
  60.7 1.5 %slice.909 = f32[64,3,512]{2,0,1:T(8,128)} slice(f32[128,3,512]{2,0,1:T(8,128)S(1)} %scatter.9), slice={[1:128:2], [0:3:1], [0:512:1]} | slice | bytes 786432 | tf_op jit(solution)/shard_map/slice | solution.py:99
  62.2 1.4 %slice.900 = f32[64,3,512]{2,0,1:T(8,128)} slice(f32[128,3,512]{2,0,1:T(8,128)S(1)} %scatter.9), slice={[0:127:2], [0:3:1], [0:512:1]} | slice | bytes 786432 | tf_op jit(solution)/shard_map/slice | solution.py:99
  63.6 1.6 %slice.994 = f32[63,3,512]{2,0,1:T(8,128)} slice(f32[128,3,512]{2,0,1:T(8,128)S(1)} %copy-done.2), slice={[2:128:2], [0:3:1], [0:512:1]} | slice | bytes 774144 | tf_op jit(solution)/shard_map/slice | solution.py:99
  65.2 1.5 %slice.901 = f32[64,3,512]{2,0,1:T(8,128)} slice(f32[128,3,512]{2,0,1:T(8,128)S(1)} %copy-done.2), slice={[1:128:2], [0:3:1], [0:512:1]} | slice | bytes 786432 | tf_op jit(solution)/shard_map/slice | solution.py:99
  66.7 1.4 %slice.897 = f32[64,3,512]{2,0,1:T(8,128)} slice(f32[128,3,512]{2,0,1:T(8,128)S(1)} %copy-done.2), slice={[0:127:2], [0:3:1], [0:512:1]} | slice | bytes 786432 | tf_op jit(solution)/shard_map/slice | solution.py:99
  68.1 1.6 %slice.990 = f32[63,3,512]{2,0,1:T(8,128)} slice(f32[128,3,512]{2,0,1:T(8,128)S(1)} %get-tuple-element.239), slice={[2:128:2], [0:3:1], [0:512:1]} | slice | bytes 774144 | tf_op jit(solution)/shard_map/slice | solution.py:99
  69.8 1.4 %slice.904 = f32[64,3,512]{2,0,1:T(8,128)} slice(f32[128,3,512]{2,0,1:T(8,128)S(1)} %get-tuple-element.239), slice={[0:127:2], [0:3:1], [0:512:1]} | slice | bytes 786432 | tf_op jit(solution)/shard_map/slice | solution.py:99
  71.2 1.4 %slice.898 = f32[64,3,512]{2,0,1:T(8,128)} slice(f32[128,3,512]{2,0,1:T(8,128)S(1)} %get-tuple-element.239), slice={[1:128:2], [0:3:1], [0:512:1]} | slice | bytes 786432 | tf_op jit(solution)/shard_map/slice | solution.py:99
  72.6 1.4 %slice.903 = f32[64,3,512]{2,0,1:T(8,128)} slice(f32[128,3,512]{2,0,1:T(8,128)S(1)} %get-tuple-element.240), slice={[0:127:2], [0:3:1], [0:512:1]} | slice | bytes 786432 | tf_op jit(solution)/shard_map/slice | solution.py:99
  74.1 1.4 %slice.896 = f32[64,3,512]{2,0,1:T(8,128)} slice(f32[128,3,512]{2,0,1:T(8,128)S(1)} %get-tuple-element.240), slice={[1:128:2], [0:3:1], [0:512:1]} | slice | bytes 786432 | tf_op jit(solution)/shard_map/slice | solution.py:99
  75.5 2.0 %multiply_subtract_fusion = (f32[64,3,512]{2,0,1:T(8,128)S(1)}, f32[64,3,512]{2,0,1:T(8,128)S(1)}, f32[64,3,512]{2,0,1:T(8,128)S(1)}, f32[64,3,512]{2,0,1:T(8,128)S(1)}) fusion(f32[64,3,512]{2,0,1:T(8,128)} %slice.898, f32[64,3,512]{2,0,1:T(8,128)} %slice.904, f32[64,3,512]{2,0,1:T(8,128)} %slice.896, f32[64,3,512]{2,0,1:T(8,128)} %slice.903, ...), kind=kLoop, calls=%fused_computation.22 | loop fusion | flops 1376256 | bytes 4718592 | tf_op jit(solution)/shard_map/sub | solution.py:52
  77.6 0.6 slice.895
  78.2 0.2 slice.913
  78.4 0.2 slice.906
  78.7 0.2 slice.905
  78.9 0.8 slice.984
  79.7 0.2 slice.914
  80.0 0.2 slice.908
  80.2 0.2 slice.988
  80.4 0.2 slice.911
  80.7 0.2 slice.907
  80.9 0.2 slice.992
  81.2 0.2 slice.919
  81.4 0.2 slice.910
  81.7 0.2 add_add_fusion.3
  84.9 0.9 copy-done.8
  85.8 0.2 add_add_fusion.2
  86.5 0.8 copy-done.6
  87.4 0.1 copy-done.5
  87.6 0.4 subtract_add_fusion
  88.2 0.2 pad.116
  88.3 0.2 pad.114
  88.5 0.2 pad.115
  88.7 0.2 fusion
  88.9 0.2 pad.117
  89.1 0.2 fusion.1
  89.3 1.7 %copy.252 = bf16[3,128,2,512]{3,2,1,0:T(2,128)(2,1)} copy(bf16[3,128,2,512]{3,1,0,2:T(8,128)(2,1)S(1)} %maximum_bitcast_fusion) | data formatting | bytes 1572864 | tf_op jit(solution)/shard_map/convert_element_type | solution.py:103
  (180 shorter events, 5.5 us)
Async XLA Ops:
  0.0 0.9 copy-start
  0.9 0.7 copy-start.9
  0.9 0.7 copy-start.10
  56.3 0.9 copy-start.1
  60.7 2.9 %copy-start.2 = (f32[128,3,512]{2,0,1:T(8,128)S(1)}, f32[128,3,512]{2,0,1:T(8,128)}, u32[]{:S(2)}) copy-start(f32[128,3,512]{2,0,1:T(8,128)} %scatter.6) | copy-start | bytes 2359300
  74.1 1.5 %copy-start.3 = (f32[64,3,512]{2,0,1:T(8,128)S(1)}, f32[64,3,512]{2,0,1:T(8,128)}, u32[]{:S(2)}) copy-start(f32[64,3,512]{2,0,1:T(8,128)} %slice.909) | copy-start | bytes 1179652
  74.1 1.5 %copy-start.4 = (f32[64,3,512]{2,0,1:T(8,128)S(1)}, f32[64,3,512]{2,0,1:T(8,128)}, u32[]{:S(2)}) copy-start(f32[64,3,512]{2,0,1:T(8,128)} %slice.900) | copy-start | bytes 1179652
  84.9 0.9 %copy-start.8 = (f32[31,3,512]{2,0,1:T(8,128)S(1)}, f32[31,3,512]{2,0,1:T(8,128)}, u32[]{:S(2)}) copy-start(f32[31,3,512]{2,0,1:T(8,128)} %slice.984) | copy-start | bytes 571396
  86.3 1.0 %copy-start.6 = (f32[63,3,512]{2,0,1:T(8,128)S(1)}, f32[63,3,512]{2,0,1:T(8,128)}, u32[]{:S(2)}) copy-start(f32[63,3,512]{2,0,1:T(8,128)} %slice.994) | copy-start | bytes 1161220
  86.3 1.1 %copy-start.7 = (f32[63,3,512]{2,0,1:T(8,128)S(1)}, f32[63,3,512]{2,0,1:T(8,128)}, u32[]{:S(2)}) copy-start(f32[63,3,512]{2,0,1:T(8,128)} %slice.990) | copy-start | bytes 1161220
  86.4 1.1 %copy-start.5 = (f32[63,3,512]{2,0,1:T(8,128)S(1)}, f32[63,3,512]{2,0,1:T(8,128)}, u32[]{:S(2)}) copy-start(f32[63,3,512]{2,0,1:T(8,128)} %slice.995) | copy-start | bytes 1161220
where the time goes:
time: 91.4 us; the launch traced here: 91 us
  blocking collectives  42.4 us (46%)
  local copies, waits for them, and re-layouts  35.6 us (39%)
  other arithmetic  11.7 us (13%)
  between operations  1.24 us (1%)
    all_gather x3, blocking collectives, gathered_once(): both, at, found = (lax.all_gather(jnp.concatenate(lines), axis), 0, {})  42.4 us
    slice x76, local copies, waits for them, and re-layouts, shards(): lax.associative_scan(compose, (dec_re, dec_im, drive_re, drive_im), axis=0)  21.8 us
    add x16, other arithmetic, compose(): lar * ebi + lai * ebr + lbi  6.03 us
    unnamed x25, local copies, waits for them, and re-layouts  5.61 us
    sub x9, other arithmetic, compose(): lar * ear - lai * eai  2.61 us

commit v1 on v0

v1 whole, which is shorter than its diff:
```python
import functools

import jax
import jax.numpy as jnp
from jax import lax
from jax.experimental import pallas as pl
from jax.experimental.pallas import tpu as pltpu
from jax.sharding import Mesh
from jax.sharding import PartitionSpec as P

LANES = 128
ROWS = 8
STEP = 16
GROUP = 8

HBM = pl.BlockSpec(memory_space=pltpu.HBM)
VMEM = pl.BlockSpec(memory_space=pltpu.VMEM)


def times(one, two):
    a, b = one
    c, d = two
    return (a * c - b * d, a * d + b * c)


def powers(base, count):
    found = [None, base]
    for n in range(2, count):
        found.append(times(found[n // 2], found[n - n // 2]))
    return found


def parity():
    return lax.broadcasted_iota(jnp.int32, (ROWS, LANES), 0) % 2 == 0


def turned(value, even):
    return jnp.where(even, -pltpu.roll(value, ROWS - 1, 0), pltpu.roll(value, 1, 0))


def doubled(rows):
    return jnp.concatenate([rows[j // 2 : j // 2 + 1] for j in range(ROWS)], axis=0)


def lane_product(value):
    for width, turns in ((1, 4), (4, 4), (16, 4), (64, 2)):
        rolled = [value] + [pltpu.roll(value, width * n, 1) for n in range(1, turns)]
        while len(rolled) > 1:
            rolled = [rolled[n] * rolled[n + 1] for n in range(0, len(rolled), 2)]
        value = rolled[0]
    return value


def minus_expm1_twice(rate):
    u = 2.0 * rate
    series = u * (1.0 - u / 2 * (1.0 - u / 3 * (1.0 - u / 4 * (1.0 - u / 5 * (1.0 - u / 6)))))
    return jnp.where(u < 0.1, series, 1.0 - jnp.exp(-u))


def first(batch, length, x_hbm, rate_hbm, phase_hbm, keep_hbm, x_ref, send_ref, start_ref, chunk_ref,
          block_ref, row_ref, small_ref, factor_ref, reach_ref, keep_ref, param_ref, own_ref, keep_all, sems):
    row, col = lax.axis_index("row"), lax.axis_index("col")
    chunks = length // STEP
    span = length * ROWS
    loads = [
        pltpu.make_async_copy(rate_hbm, param_ref.at[0], sems.at[0]),
        pltpu.make_async_copy(phase_hbm, param_ref.at[1], sems.at[1]),
        pltpu.make_async_copy(keep_hbm.at[row * GROUP + col], own_ref, sems.at[2]),
        pltpu.make_async_copy(keep_hbm, keep_all, sems.at[3]),
    ] + [
        pltpu.make_async_copy(x_hbm.at[pl.ds(s * span, span)], x_ref.at[pl.ds(s * span, span)], sems.at[4 + s])
        for s in range(batch)
    ]
    for load in loads:
        load.start()
    even = parity()
    loads[0].wait()
    loads[1].wait()
    rate, phase = doubled(param_ref[0]), doubled(param_ref[1])
    magnitude = jnp.exp(-rate)
    one = jnp.ones_like(rate)
    zero = jnp.zeros_like(rate)
    lam = (magnitude * jnp.cos(phase), magnitude * jnp.sin(phase))
    step = powers(lam, STEP + 1)
    chunk = powers(step[STEP], chunks + 1)
    block = powers(chunk[chunks], GROUP + 1)
    line = powers(block[GROUP], GROUP)
    small_ref[0], small_ref[1] = lam
    small_ref[2] = jnp.sqrt(minus_expm1_twice(rate))
    for ref, found, before in ((chunk_ref, chunk[:chunks], 0), (block_ref, block[:GROUP], GROUP), (row_ref, line, GROUP)):
        for part in range(2):
            for n in range(before):
                ref[part, n] = zero
            ref[part, before] = zero if part else one
            for n in range(1, len(found)):
                ref[part, before + n] = found[n][part]
    loads[3].wait()
    products = [lane_product(keep_all[row * GROUP + m]) for m in range(GROUP)]
    for line_at in range(GROUP):
        product = keep_all[line_at * GROUP]
        for m in range(1, GROUP):
            product = product * keep_all[line_at * GROUP + m]
        products.append(lane_product(product))
    for n, product in enumerate(products):
        for s in range(batch):
            factor_ref[n, s] = jnp.broadcast_to(product[s : s + 1], (ROWS, LANES))
    loads[2].wait()
    for s in range(batch):
        loads[4 + s].wait()
        direct, cross, decay = [None] * chunks, [None] * chunks, [None] * chunks
        for i in range(STEP):
            for k in range(chunks):
                t = k * STEP + i
                x = x_ref[pl.ds(s * span + t * ROWS, ROWS)].astype(jnp.float32)
                kept = jnp.full((ROWS, LANES), own_ref[s, t], jnp.float32)
                keep_ref[pl.ds(s * length + t, 1)] = kept[:1]
                n = STEP - 1 - i
                dir_x, cross_x = (x, None) if n == 0 else (step[n][0] * x, step[n][1] * x)
                if i == 0:
                    direct[k], cross[k], decay[k] = dir_x, cross_x, kept
                else:
                    direct[k] = kept * direct[k] + dir_x
                    cross[k] = kept * cross[k] if cross_x is None else kept * cross[k] + cross_x
                    decay[k] = kept * decay[k]
        state, reach = zero, one
        for k in range(chunks):
            start_ref[s, k] = state
            reach_ref[pl.ds(s * chunks + k, 1)] = reach[:1]
            end = direct[k] + turned(cross[k], even)
            if k:
                end = decay[k] * (step[STEP][0] * state + step[STEP][1] * turned(state, even)) + end
            state, reach = end, reach * decay[k]
        for n in range(GROUP):
            send_ref[n, s] = state


def second(batch, got_ref, block_ref, factor_ref, send_ref):
    even = parity()
    for s in range(batch):
        direct = cross = None
        for m in range(GROUP):
            x = got_ref[m, s]
            a, b = block_ref[0, 2 * GROUP - 1 - m], block_ref[1, 2 * GROUP - 1 - m]
            if m == 0:
                direct, cross = a * x, b * x
            else:
                direct = factor_ref[m, s] * direct + a * x
                cross = factor_ref[m, s] * cross + b * x
        total = direct + turned(cross, even)
        for n in range(GROUP):
            send_ref[n, s] = total


def before_me(me, got_ref, power_ref, factor_ref, at, s, even):
    direct = cross = jnp.zeros((ROWS, LANES), jnp.float32)
    reach = jnp.ones((ROWS, LANES), jnp.float32)
    for m in range(GROUP):
        n = GROUP - 1 + me - m
        kept = jnp.where(m < me, factor_ref[at + m, s], 1.0)
        direct = kept * direct + power_ref[0, n] * got_ref[m, s]
        cross = kept * cross + power_ref[1, n] * got_ref[m, s]
        reach = kept * reach
    return direct + turned(cross, even), reach


def third(batch, length, x_ref, near_ref, far_ref, start_ref, chunk_ref, block_ref, row_ref, small_ref,
          factor_ref, reach_ref, keep_ref, y_hbm, y_ref, sems):
    row, col = lax.axis_index("row"), lax.axis_index("col")
    chunks = length // STEP
    span = length * ROWS
    even = parity()
    carries = []
    for s in range(batch):
        inside, reach = before_me(col, near_ref, block_ref, factor_ref, 0, s, even)
        lines, _ = before_me(row, far_ref, row_ref, factor_ref, GROUP, s, even)
        a, b = block_ref[0, GROUP + col], block_ref[1, GROUP + col]
        carries.append(reach * (a * lines + b * turned(lines, even)) + inside)
    lam_re, gamma = small_ref[0], small_ref[2]
    lam_im = jnp.where(even, -small_ref[1], small_ref[1])
    stores = []
    for s in range(batch):
        carry, spun = carries[s], turned(carries[s], even)
        state = [
            start_ref[s, k]
            + jnp.broadcast_to(reach_ref[pl.ds(s * chunks + k, 1)], (ROWS, LANES))
            * (chunk_ref[0, k] * carry + chunk_ref[1, k] * spun)
            for k in range(chunks)
        ]
        for i in range(STEP):
            for k in range(chunks):
                t = k * STEP + i
                h = state[k]
                swapped = jnp.where(even, pltpu.roll(h, ROWS - 1, 0), pltpu.roll(h, 1, 0))
                kept = jnp.broadcast_to(keep_ref[pl.ds(s * length + t, 1)], (ROWS, LANES))
                x = x_ref[pl.ds(s * span + t * ROWS, ROWS)].astype(jnp.float32)
                state[k] = kept * (lam_re * h + lam_im * swapped) + x
                y_ref[pl.ds(s * span + t * ROWS, ROWS)] = (gamma * state[k]).astype(jnp.bfloat16)
        store = pltpu.make_async_copy(y_ref.at[pl.ds(s * span, span)], y_hbm.at[pl.ds(s * span, span)], sems.at[s])
        store.start()
        stores.append(store)
    for store in stores:
        store.wait()


def shards(inputs, decay_rate, phase, keep):
    batch, length, parts, width = inputs.shape
    tiles = width // LANES
    blocks = keep.shape[1] // length
    chunks = length // STEP
    f32 = functools.partial(jax.ShapeDtypeStruct, dtype=jnp.float32)
    total = batch * length * ROWS
    x = inputs.reshape(batch, length, parts, tiles, LANES).transpose(0, 1, 3, 2, 4).reshape(total, LANES)
    kept = keep.reshape(batch, blocks, length).transpose(1, 0, 2)
    exchange = f32((GROUP, batch, ROWS, LANES))
    x, send, start, chunk, block, line, small, factor, reach, keeps = pl.pallas_call(
        functools.partial(first, batch, length),
        out_shape=[
            jax.ShapeDtypeStruct((total, LANES), jnp.bfloat16),
            exchange,
            f32((batch, chunks, ROWS, LANES)),
            f32((2, chunks, ROWS, LANES)),
            f32((2, 2 * GROUP, ROWS, LANES)),
            f32((2, 2 * GROUP, ROWS, LANES)),
            f32((3, ROWS, LANES)),
            f32((2 * GROUP, batch, ROWS, LANES)),
            f32((batch * chunks, LANES)),
            f32((batch * length, LANES)),
        ],
        in_specs=[HBM] * 4,
        out_specs=[VMEM] * 10,
        scratch_shapes=[
            pltpu.VMEM((2, tiles, LANES), jnp.float32),
            pltpu.SMEM((batch, LANES), jnp.float32),
            pltpu.VMEM((blocks, batch, LANES), jnp.float32),
            pltpu.SemaphoreType.DMA((4 + batch,)),
        ],
    )(x, decay_rate.reshape(tiles, LANES), phase.reshape(tiles, LANES), kept)

    def swap(value, axis):
        flat = value.reshape(GROUP, batch * ROWS, LANES)
        return lax.all_to_all(flat, axis, 0, 0, tiled=True).reshape(value.shape)

    near = swap(send, "col")
    totals = pl.pallas_call(
        functools.partial(second, batch),
        out_shape=exchange,
        in_specs=[VMEM] * 3,
        out_specs=VMEM,
    )(near, block, factor)
    far = swap(totals, "row")
    y = pl.pallas_call(
        functools.partial(third, batch, length),
        out_shape=jax.ShapeDtypeStruct((total, LANES), jnp.bfloat16),
        in_specs=[VMEM] * 11,
        out_specs=HBM,
        scratch_shapes=[
            pltpu.VMEM((total, LANES), jnp.bfloat16),
            pltpu.SemaphoreType.DMA((batch,)),
        ],
    )(x, near, far, start, chunk, block, line, small, factor, reach, keeps)
    y = y.reshape(batch, length, tiles, parts, LANES).transpose(0, 1, 3, 2, 4)
    return y.reshape(inputs.shape)


def solution(mesh):
    split = Mesh(mesh.devices.reshape(mesh.shape["chan"], GROUP, GROUP), ("chan", "row", "col"))
    seq = ("row", "col")
    return jax.shard_map(
        shards,
        mesh=split,
        in_specs=(P(None, seq, None, "chan"), P("chan"), P("chan"), P()),
        out_specs=P(None, seq, None, "chan"),
        check_vma=False,
    )
```

time: 91.4 us -> 35.1 us (0.38)
  the two profiles are of different devices: /device:TPU:4 before, /device:TPU:1 now
where the time goes in v1:
time: 35.1 us; the launch traced here: 34.8 us
  blocking collectives  27.2 us (77%)
  Pallas kernels  7.55 us (22%)
    all_to_all x2, blocking collectives, swap(): return lax.all_to_all(flat, axis, 0, 0, tiled=True).reshape(value.shape)  27.2 us
    pallas_call x1, Pallas kernels, shards(): pl.pallas_call(functools.partial(first, batch, length), out_shape=[jax.Sh...  2.94 us
    pallas_call x1, Pallas kernels, shards(): pl.pallas_call(functools.partial(third, batch, length), out_shape=jax.Sha...  2.9 us
    pallas_call x1, Pallas kernels, shards(): pl.pallas_call(functools.partial(second, batch), out_shape=exchange, in_s...  1.71 us

profile of v1, /device:TPU:1, one launch (start us, length us, event | category | flops | bytes accessed | tf_op | source)
XLA Modules:
  0.0 34.8 jit_solution(16862147762661518199)
XLA Ops:
  0.0 2.9 %shard_map.46 = (bf16[3072,128]{1,0:T(8,128)(2,1)}, f32[8,3,8,128]{3,2,1,0:T(8,128)}, f32[3,8,8,128]{3,2,1,0:T(8,128)}, f32[2,8,8,128]{3,2,1,0:T(8,128)}, f32[2,...) custom-call(bf16[3072,128]{1,0:T(8,128)(2,1)} %bitcast.21, ...), custom_call_target="tpu_custom_call" | custom-call | tf_op jit(solution)/shard_map/pallas_call | solution.py:215
  2.9 15.8 %all_to_all.10 = f32[8,24,128]{2,1,0:T(8,128)} all-to-all(f32[8,24,128]{2,1,0:T(8,128)} %bitcast.25), channel_id=1, replica_groups=mesh['chan'=8,'row'=8,'col'=8] {'col'}, dimensions={0} | all-to-all | bytes 196608 | tf_op jit(solution)/shard_map/all_to_all | solution.py:241
  18.7 1.7 %shard_map.47 = f32[8,3,8,128]{3,2,1,0:T(8,128)} custom-call(f32[8,3,8,128]{3,2,1,0:T(8,128)} %bitcast.19, f32[2,16,8,128]{3,2,1,0:T(8,128)} %get-tuple-element.17.block_ref, f32[16,3,8,128]{3,2,1,0:T(8,128)} %get-tuple-element.18.factor_ref), custom_call_target="tpu_custom_call" | custom-call | tf_op jit(solution)/shard_map/pallas_call | solution.py:244
  20.4 11.4 %all_to_all.11 = f32[8,24,128]{2,1,0:T(8,128)} all-to-all(f32[8,24,128]{2,1,0:T(8,128)} %bitcast.23), channel_id=1, replica_groups=mesh['chan'=8,'row'=8,'col'=8] {'row'}, dimensions={0} | all-to-all | bytes 196608 | tf_op jit(solution)/shard_map/all_to_all | solution.py:241
  31.8 2.9 %shard_map.48 = bf16[3072,128]{1,0:T(8,128)(2,1)} custom-call(bf16[3072,128]{1,0:T(8,128)(2,1)} %get-tuple-element.15.x_ref, f32[8,3,8,128]{3,2,1,0:T(8,128)} %bitcast.20, f32[8,3,8,128]{3,2,1,0:T(8,128)} %bitcast.22, f32[3,8,8,128]{3,2,1,0:T(8,128)} %get-tuple-element.19.start_ref, f32[2,8,8,128]{3,2,1,0:T(8,128)} %get-tuple-element.20.chunk_ref, ...), custom_call_target="tpu_custom_call" | custom-call | tf_op jit(solution)/shard_map/pallas_call | solution.py:251

commit v2 on v1

--- a/solution.py
+++ b/solution.py
@@ -10,6 +10,7 @@
 
 LANES = 128
 ROWS = 8
+LIMIT = pltpu.CompilerParams(vmem_limit_bytes=8388608)
 STEP = 16
 GROUP = 8
 
@@ -226,6 +227,7 @@
             f32((batch * chunks, LANES)),
             f32((batch * length, LANES)),
         ],
+        compiler_params=LIMIT,
         in_specs=[HBM] * 4,
         out_specs=[VMEM] * 10,
         scratch_shapes=[
@@ -234,7 +236,7 @@
             pltpu.VMEM((blocks, batch, LANES), jnp.float32),
             pltpu.SemaphoreType.DMA((4 + batch,)),
         ],
-    )(x, decay_rate.reshape(tiles, LANES), phase.reshape(tiles, LANES), kept)
+    )(*(pltpu.with_memory_space_constraint(v, pltpu.HBM) for v in (x, decay_rate.reshape(tiles, LANES), phase.reshape(tiles, LANES), kept)))
 
     def swap(value, axis):
         flat = value.reshape(GROUP, batch * ROWS, LANES)
@@ -244,6 +246,7 @@
     totals = pl.pallas_call(
         functools.partial(second, batch),
         out_shape=exchange,
+        compiler_params=LIMIT,
         in_specs=[VMEM] * 3,
         out_specs=VMEM,
     )(near, block, factor)
@@ -251,6 +254,7 @@
     y = pl.pallas_call(
         functools.partial(third, batch, length),
         out_shape=jax.ShapeDtypeStruct((total, LANES), jnp.bfloat16),
+        compiler_params=LIMIT,
         in_specs=[VMEM] * 11,
         out_specs=HBM,
         scratch_shapes=[

time: 35.1 us -> 29.1 us (0.83)
  the two profiles are of different devices: /device:TPU:1 before, /device:TPU:448 now
where the time goes in v2:
time: 29.1 us; the launch traced here: 28.9 us
  blocking collectives  25.5 us (88%)
  Pallas kernels  3.4 us (12%)
    all_to_all x2, blocking collectives, swap(): return lax.all_to_all(flat, axis, 0, 0, tiled=True).reshape(value.shape)  25.5 us
    pallas_call x1, Pallas kernels, shards(): pl.pallas_call(functools.partial(first, batch, length), out_shape=[jax.Sh...  1.94 us
    pallas_call x1, Pallas kernels, shards(): pl.pallas_call(functools.partial(third, batch, length), out_shape=jax.Sha...  1.42 us

profile of v2, /device:TPU:448, one launch (start us, length us, event | category | flops | bytes accessed | tf_op | source)
XLA Modules:
  0.0 28.9 jit_solution(3846262821153048626)
XLA Ops:
  0.0 1.9 %shard_map.46 = (bf16[3072,128]{1,0:T(8,128)(2,1)S(1)}, f32[8,3,8,128]{3,2,1,0:T(8,128)S(1)}, f32[3,8,8,128]{3,2,1,0:T(8,128)S(1)}, f32[2,8,8,128]{3,2,1,0:T(8,1...) custom-call(bf16[3072,128]{1,0:T(8,128)(2,1)} %bitcast.24, ...), custom_call_target="tpu_custom_call" | custom-call | tf_op jit(solution)/shard_map/pallas_call | solution.py:216
  1.9 9.9 %all_to_all.10 = f32[8,24,128]{2,1,0:T(8,128)S(1)} all-to-all(f32[8,24,128]{2,1,0:T(8,128)S(1)} %bitcast.23), channel_id=1, replica_groups=mesh['chan'=8,'row'=8,'col'=8] {'col'}, dimensions={0} | all-to-all | bytes 196608 | tf_op jit(solution)/shard_map/all_to_all | solution.py:243
  11.9 15.6 %all_to_all.11 = f32[8,24,128]{2,1,0:T(8,128)S(1)} all-to-all(f32[8,24,128]{2,1,0:T(8,128)S(1)} %bitcast.22), channel_id=1, replica_groups=mesh['chan'=8,'row'=8,'col'=8] {'row'}, dimensions={0} | all-to-all | bytes 196608 | tf_op jit(solution)/shard_map/all_to_all | solution.py:243
  27.5 1.4 %shard_map.48 = bf16[3072,128]{1,0:T(8,128)(2,1)} custom-call(bf16[3072,128]{1,0:T(8,128)(2,1)S(1)} %get-tuple-element.15.x_ref, f32[8,3,8,128]{3,2,1,0:T(8,128)S(1)} %bitcast.20, f32[8,3,8,128]{3,2,1,0:T(8,128)S(1)} %bitcast.21, f32[3,8,8,128]{3,2,1,0:T(8,128)S(1)} %get-tuple-element.19.start_ref, f32[2,8,8,128]{3,2,1,0:T(8,128)S(1)} %get-tuple-element.20.chunk_ref, ...), custom_call_target="tpu_custom_call" | custom-call | tf_op jit(solution)/shard_map/pallas_call | solution.py:254
  (1 shorter events, 0.0 us)

commit v3 on v1

v3 whole, which is shorter than its diff:
```python
import functools

import jax
import jax.numpy as jnp
from jax import lax
from jax.experimental import pallas as pl
from jax.experimental.pallas import tpu as pltpu
from jax.sharding import Mesh
from jax.sharding import PartitionSpec as P

LANES = 128
ROWS = 8
STEP = 16
NEAR = 16
FAR = 4
WIDE = 8
SENDS = (
    ((0, 1, 0),),
    ((0, 3, 0),),
    ((0, 2, 1), (1, 3, 1)),
    ((1, 2, 0), (2, 3, 0)),
)

HBM = pl.BlockSpec(memory_space=pltpu.HBM)
VMEM = pl.BlockSpec(memory_space=pltpu.VMEM)
LIMIT = pltpu.CompilerParams(vmem_limit_bytes=8 * 1024 * 1024)


def times(one, two):
    a, b = one
    c, d = two
    return (a * c - b * d, a * d + b * c)


def powers(base, count):
    found = [None, base]
    for n in range(2, count):
        found.append(times(found[n // 2], found[n - n // 2]))
    return found


def places():
    return lax.broadcasted_iota(jnp.int32, (ROWS, LANES), 0)


def sign():
    return jnp.where(places() % 2 == 0, -1.0, 1.0)


def swapped(value):
    return jnp.take_along_axis(value, places() ^ 1, axis=0, mode="promise_in_bounds")


def spread(row):
    return jnp.broadcast_to(row, (ROWS, LANES))


def doubled(rows):
    return jnp.concatenate([rows[j // 2 : j // 2 + 1] for j in range(ROWS)], axis=0)


def lane_product(value):
    for width, turns in ((1, 4), (4, 4), (16, 4), (64, 2)):
        rolled = [value] + [pltpu.roll(value, width * n, 1) for n in range(1, turns)]
        while len(rolled) > 1:
            rolled = [rolled[n] * rolled[n + 1] for n in range(0, len(rolled), 2)]
        value = rolled[0]
    return value


def minus_expm1_twice(rate):
    u = 2.0 * rate
    series = u * (1.0 - u / 2 * (1.0 - u / 3 * (1.0 - u / 4 * (1.0 - u / 5 * (1.0 - u / 6)))))
    return jnp.where(u < 0.1, series, 1.0 - jnp.exp(-u))


def first(batch, length, x_hbm, rate_hbm, phase_hbm, keep_hbm, local_ref, send_ref, start_ref, chunk_ref, step_ref,
          reach_ref, decay_ref, total_ref, inside_ref, lines_ref, x_ref, keep_ref, param_ref, own_ref, block_ref,
          run_ref, sems):
    me = lax.axis_index("seq")
    run, at = me // NEAR, me % NEAR
    chunks = length // STEP
    span = length * ROWS
    pieces = [
        pltpu.make_async_copy(x_hbm.at[pl.ds(s * span, span)], x_ref.at[pl.ds(s * span, span)], sems.at[4 + s])
        for s in range(batch)
    ]
    loads = [
        pltpu.make_async_copy(rate_hbm, param_ref.at[0], sems.at[0]),
        pltpu.make_async_copy(phase_hbm, param_ref.at[1], sems.at[1]),
        pltpu.make_async_copy(keep_hbm.at[me], own_ref, sems.at[2]),
        pltpu.make_async_copy(keep_hbm, keep_ref, sems.at[3]),
    ]
    for load in loads[:3] + pieces[:1] + loads[3:] + pieces[1:]:
        load.start()
    flip = sign()
    loads[0].wait()
    loads[1].wait()
    rate, phase = doubled(param_ref[0]), doubled(param_ref[1])
    magnitude = jnp.exp(-rate)
    one, zero = jnp.ones_like(rate), jnp.zeros_like(rate)
    lam = (magnitude * jnp.cos(phase), magnitude * jnp.sin(phase))
    gamma = jnp.sqrt(minus_expm1_twice(rate))
    step = powers(lam, STEP + 1)
    chunk = powers(step[STEP], chunks + 1)
    block = powers(chunk[chunks], NEAR + 1)
    run_ref[0], run_ref[1] = block[NEAR]
    for part in range(2):
        for n in range(STEP):
            step_ref[part, n] = step[n + 1][part]
        for n in range(NEAR):
            block_ref[part, n] = zero
        block_ref[part, NEAR] = zero if part else one
        for n in range(1, NEAR):
            block_ref[part, NEAR + n] = block[n][part]
        chunk_ref[part, 0] = zero if part else one
        for n in range(1, chunks):
            chunk_ref[part, n] = chunk[n][part]
    lam_re, lam_im = lam[0], lam[1] * flip
    jump_re, jump_im = step[STEP][0], step[STEP][1] * flip

    def scan(s):
        state, decay = [None] * chunks, [None] * chunks
        for i in range(STEP):
            for k in range(chunks):
                t = k * STEP + i
                x = gamma * x_ref[pl.ds(s * span + t * ROWS, ROWS)].astype(jnp.float32)
                kept = jnp.full((ROWS, LANES), own_ref[s, t], jnp.float32)
                if i == 0:
                    state[k], decay[k] = x, kept
                else:
                    h = state[k]
                    state[k] = kept * (lam_re * h + lam_im * swapped(h)) + x
                    decay[k] = kept * decay[k]
                local_ref[s, t] = state[k]
                decay_ref[pl.ds(s * length + t, 1)] = decay[k][:1]
        return state, decay

    def chain(s, ends, decays):
        state, reach = zero, one
        for k in range(chunks):
            start_ref[s, k] = state
            reach_ref[pl.ds(s * chunks + k, 1)] = reach[:1]
            if k:
                state = decays[k] * (jump_re * state + jump_im * swapped(state)) + ends[k]
            else:
                state = ends[k]
            reach = reach * decays[k]
        for n in range(NEAR):
            send_ref[n, s] = state

    def block_products():
        near = [lane_product(keep_ref[run * NEAR + m]) for m in range(NEAR)]
        far = []
        for n in range(FAR):
            product = keep_ref[n * NEAR]
            for m in range(1, NEAR):
                product = product * keep_ref[n * NEAR + m]
            far.append(lane_product(product))
        return near, far

    def weights(near, far):
        after = jnp.ones((batch, LANES), jnp.float32)
        for m in reversed(range(NEAR)):
            for s in range(batch):
                factor = spread(after[s : s + 1])
                for part in range(2):
                    total_ref[part, m, s] = factor * block_ref[part, 2 * NEAR - 1 - m]
            after = after * near[m]
        after = jnp.ones((batch, LANES), jnp.float32)
        for m in reversed(range(NEAR)):
            for s in range(batch):
                factor = spread(after[s : s + 1])
                for part in range(2):
                    inside_ref[part, m, s] = factor * block_ref[part, NEAR - 1 + at - m]
            after = after * jnp.where(m < at, near[m], 1.0)
        weight = (block_ref[0, NEAR + at], block_ref[1, NEAR + at])
        jump = (run_ref[0], run_ref[1])
        for d in range(1, FAR):
            for s in range(batch):
                factor = spread(after[s : s + 1])
                for part in range(2):
                    lines_ref[part, d - 1, s] = factor * weight[part]
            if d < FAR - 1:
                before = far[0]
                for m in range(1, FAR):
                    before = jnp.where(run - d == m, far[m], before)
                after = after * before
                weight = times(weight, jump)

    loads[2].wait()
    pieces[0].wait()
    found = scan(0)
    loads[3].wait()
    for s in range(1, batch):
        pieces[s].wait()
        if s == 1:
            products = block_products()
        if s == batch - 1:
            weights(*products)
        chain(s - 1, *found)
        found = scan(s)
    chain(batch - 1, *found)


def gathered(terms, flip):
    direct = cross = None
    for real, imag, x in terms:
        one, two = real * x, imag * x
        direct, cross = (one, two) if direct is None else (direct + one, cross + two)
    return direct + flip * swapped(cross)


def second(batch, got_ref, total_ref, send_ref):
    flip = sign()
    for s in range(batch):
        send_ref[s] = gathered([(total_ref[0, m, s], total_ref[1, m, s], got_ref[m, s]) for m in range(NEAR)], flip)


def third(batch, length, local_ref, near_ref, start_ref, chunk_ref, step_ref, reach_ref, decay_ref, inside_ref, lines_ref,
          *rest):
    far_refs, (y_hbm, y_ref, sems) = rest[: len(SENDS)], rest[len(SENDS) :]
    run = lax.axis_index("seq") // NEAR
    chunks = length // STEP
    part = chunks // 2
    size = part * STEP * ROWS
    flip = sign()
    stores = []
    for s in range(batch):
        terms = [(inside_ref[0, m, s], inside_ref[1, m, s], near_ref[m, s]) for m in range(NEAR)]
        for sends, far_ref in zip(SENDS, reversed(far_refs)):
            d = sum(jnp.where(run == to, to - at - 1, 0) for at, to, _ in sends)
            terms.append((lines_ref[0, d, s], lines_ref[1, d, s], far_ref[s]))
        carry = gathered(terms, flip)
        spun = flip * swapped(carry)
        for half in range(2):
            for k in range(half * part, half * part + part):
                entry = start_ref[s, k] + spread(reach_ref[pl.ds(s * chunks + k, 1)]) * (
                    chunk_ref[0, k] * carry + chunk_ref[1, k] * spun
                )
                turned = flip * swapped(entry)
                for i in range(STEP):
                    t = k * STEP + i
                    decay = spread(decay_ref[pl.ds(s * length + t, 1)])
                    state = local_ref[s, t] + decay * (step_ref[0, i] * entry + step_ref[1, i] * turned)
                    y_ref[pl.ds((s * length + t) * ROWS, ROWS)] = state.astype(jnp.bfloat16)
            rows = pl.ds((2 * s + half) * size, size)
            store = pltpu.make_async_copy(y_ref.at[rows], y_hbm.at[rows], sems.at[2 * s + half])
            store.start()
            stores.append(store)
    for store in stores:
        store.wait()


def shards(inputs, decay_rate, phase, keep):
    batch, length, parts, width = inputs.shape
    tiles = width // LANES
    blocks = keep.shape[1] // length
    chunks = length // STEP
    f32 = functools.partial(jax.ShapeDtypeStruct, dtype=jnp.float32)
    tile = (ROWS, LANES)
    total = batch * length * ROWS
    x = inputs.reshape(batch, length, parts, tiles, LANES).transpose(0, 1, 3, 2, 4).reshape(total, LANES)
    kept = keep.reshape(batch, blocks, length).transpose(1, 0, 2)
    given = (x, decay_rate.reshape(tiles, LANES), phase.reshape(tiles, LANES), kept)
    local, send, start, chunk, step, reach, decay, totals, inside, lines = pl.pallas_call(
        functools.partial(first, batch, length),
        out_shape=[
            f32((batch, length, *tile)),
            f32((NEAR, batch, *tile)),
            f32((batch, chunks, *tile)),
            f32((2, chunks, *tile)),
            f32((2, STEP, *tile)),
            f32((batch * chunks, LANES)),
            f32((batch * length, LANES)),
            f32((2, NEAR, batch, *tile)),
            f32((2, NEAR, batch, *tile)),
            f32((2, FAR - 1, batch, *tile)),
        ],
        in_specs=[HBM] * 4,
        out_specs=[VMEM] * 10,
        scratch_shapes=[
            pltpu.VMEM((total, LANES), jnp.bfloat16),
            pltpu.VMEM((blocks, batch, LANES), jnp.float32),
            pltpu.VMEM((2, tiles, LANES), jnp.float32),
            pltpu.SMEM((batch, LANES), jnp.float32),
            pltpu.VMEM((2, 2 * NEAR, *tile), jnp.float32),
            pltpu.VMEM((2, *tile), jnp.float32),
            pltpu.SemaphoreType.DMA((4 + batch,)),
        ],
        compiler_params=LIMIT,
    )(*(pltpu.with_memory_space_constraint(value, pltpu.HBM) for value in given))

    runs = range(blocks // NEAR)
    near = lax.all_to_all(
        send.reshape(NEAR, batch * ROWS, LANES),
        "seq",
        0,
        0,
        axis_index_groups=[[run * NEAR + m for m in range(NEAR)] for run in runs],
        tiled=True,
    ).reshape(send.shape)
    sums = pl.pallas_call(
        functools.partial(second, batch),
        out_shape=f32((batch, *tile)),
        in_specs=[VMEM] * 2,
        out_specs=VMEM,
        compiler_params=LIMIT,
    )(near, totals)
    flat = sums.reshape(batch * ROWS, LANES)
    far = []
    for sends in SENDS:
        pairs = [
            (at * NEAR + m, to * NEAR + (m + cross * WIDE) % NEAR) for at, to, cross in sends for m in range(NEAR)
        ]
        far.append(lax.ppermute(flat, "seq", pairs).reshape(sums.shape))
    y = pl.pallas_call(
        functools.partial(third, batch, length),
        out_shape=jax.ShapeDtypeStruct((total, LANES), jnp.bfloat16),
        in_specs=[VMEM] * (9 + len(SENDS)),
        out_specs=HBM,
        scratch_shapes=[
            pltpu.VMEM((total, LANES), jnp.bfloat16),
            pltpu.SemaphoreType.DMA((2 * batch,)),
        ],
        compiler_params=LIMIT,
    )(local, near, start, chunk, step, reach, decay, inside, lines, *reversed(far))
    y = y.reshape(batch, length, tiles, parts, LANES).transpose(0, 1, 3, 2, 4)
    return y.reshape(inputs.shape)


def solution(mesh):
    split = Mesh(mesh.devices, ("chan", "seq"))
    return jax.shard_map(
        shards,
        mesh=split,
        in_specs=(P(None, "seq", None, "chan"), P("chan"), P("chan"), P()),
        out_specs=P(None, "seq", None, "chan"),
        check_vma=False,
    )
```

time: 35.1 us -> 26.2 us (0.75)
  the two profiles are of different devices: /device:TPU:1 before, /device:TPU:488 now
where the time goes in v3:
time: 26.2 us; the launch traced here: 26 us
  blocking collectives  11.6 us (44%)
  starting transfers between devices  5.94 us (23%)
  waiting for transfers between devices  5.12 us (20%)
  Pallas kernels  3.23 us (12%)
    all_to_all x1, blocking collectives, shards(): lax.all_to_all(send.reshape(NEAR, batch * ROWS, LANES), 'seq', 0, 0, axis...  11.6 us
    ppermute x4, starting transfers between devices, shards(): far.append(lax.ppermute(flat, 'seq', pairs).reshape(sums.shape))  5.94 us
    ppermute x4, waiting for transfers between devices, shards(): far.append(lax.ppermute(flat, 'seq', pairs).reshape(sums.shape))  5.12 us
    pallas_call x1, Pallas kernels, shards(): pl.pallas_call(functools.partial(first, batch, length), out_shape=[f32((b...  1.99 us
    pallas_call x1, Pallas kernels, shards(): pl.pallas_call(functools.partial(third, batch, length), out_shape=jax.Sha...  1.2 us
  transfers between devices with their start and end apart: 4, of which 2 were waited for; matrix products, arithmetic and copies ran while one was open for 0% of the time, Pallas kernels for 0%

profile of v3, /device:TPU:488, one launch (start us, length us, event | category | flops | bytes accessed | tf_op | source)
XLA Modules:
  0.0 26.0 jit_solution(11225714396220168591)
XLA Ops:
  0.0 2.0 %shard_map.46 = (f32[3,128,8,128]{3,2,1,0:T(8,128)S(1)}, f32[16,3,8,128]{3,2,1,0:T(8,128)S(1)}, f32[3,8,8,128]{3,2,1,0:T(8,128)S(1)}, f32[2,8,8,128]{3,2,1,0:T(8...) custom-call(bf16[3072,128]{1,0:T(8,128)(2,1)} %bitcast.33, ...), custom_call_target="tpu_custom_call" | custom-call | tf_op jit(solution)/shard_map/pallas_call | solution.py:266
  2.0 11.6 %all_to_all.5 = f32[16,24,128]{2,1,0:T(8,128)S(1)} all-to-all(f32[16,24,128]{2,1,0:T(8,128)S(1)} %bitcast.24), channel_id=1, replica_groups={{0,1,2,3,4,5,6,7,8,9,10,11,12,13,14,15},{16,17,18,19,20,21,22,23,24,25,..., dimensions={0} | all-to-all | bytes 393216 | tf_op jit(solution)/shard_map/all_to_all | solution.py:295
  13.7 0.7 %collective-permute-start.3 = (f32[24,128]{1,0:T(8,128)S(1)}, f32[24,128]{1,0:T(8,128)S(1)}, u32[]{:S(2)}, u32[]{:S(2)}) collective-permute-start(f32[24,128]{1,0:T(8,128)S(1)} %bitcast.25), channel_id=1, source_target_pairs={{0,16},{1,17},{2,18},{3,19},{4,20},{5,21},{6,22},{7,23},{8,24},{9,... | collective-permute-start | bytes 36872 | tf_op jit(solution)/shard_map/ppermute | solution.py:316
  14.4 0.7 %collective-permute-start.2 = (f32[24,128]{1,0:T(8,128)S(1)}, f32[24,128]{1,0:T(8,128)S(1)}, u32[]{:S(2)}, u32[]{:S(2)}) collective-permute-start(f32[24,128]{1,0:T(8,128)S(1)} %bitcast.26), channel_id=1, source_target_pairs={{0,48},{1,49},{2,50},{3,51},{4,52},{5,53},{6,54},{7,55},{8,56},{9,... | collective-permute-start | bytes 36872 | tf_op jit(solution)/shard_map/ppermute | solution.py:316
  15.0 1.3 %collective-permute-start.1 = (f32[24,128]{1,0:T(8,128)S(1)}, f32[24,128]{1,0:T(8,128)S(1)}, u32[]{:S(2)}, u32[]{:S(2)}) collective-permute-start(f32[24,128]{1,0:T(8,128)S(1)} %bitcast.27), channel_id=1, source_target_pairs={{0,40},{1,41},{2,42},{3,43},{4,44},{5,45},{6,46},{7,47},{8,32},{9,... | collective-permute-start | bytes 36872 | tf_op jit(solution)/shard_map/ppermute | solution.py:316
  16.3 3.3 %collective-permute-start = (f32[24,128]{1,0:T(8,128)S(1)}, f32[24,128]{1,0:T(8,128)S(1)}, u32[]{:S(2)}, u32[]{:S(2)}) collective-permute-start(f32[24,128]{1,0:T(8,128)S(1)} %bitcast.28), channel_id=1, source_target_pairs={{16,32},{17,33},{18,34},{19,35},{20,36},{21,37},{22,38},{23,39},{2... | collective-permute-start | bytes 36872 | tf_op jit(solution)/shard_map/ppermute | solution.py:316
  19.7 0.0 collective-permute-done.3
  19.7 0.0 collective-permute-done.2
  19.7 3.9 %collective-permute-done.1 = f32[24,128]{1,0:T(8,128)S(1)} collective-permute-done((f32[24,128]{1,0:T(8,128)S(1)}, f32[24,128]{1,0:T(8,128)S(1)}, u32[]{:S(2)}, u32[]{:S(2)}) %collective-permute-start.1) | collective-permute-done | bytes 12320 | tf_op jit(solution)/shard_map/ppermute | solution.py:316
  23.6 1.2 %collective-permute-done = f32[24,128]{1,0:T(8,128)S(1)} collective-permute-done((f32[24,128]{1,0:T(8,128)S(1)}, f32[24,128]{1,0:T(8,128)S(1)}, u32[]{:S(2)}, u32[]{:S(2)}) %collective-permute-start) | collective-permute-done | bytes 12320 | tf_op jit(solution)/shard_map/ppermute | solution.py:316
  24.8 1.2 %shard_map.48 = bf16[3072,128]{1,0:T(8,128)(2,1)} custom-call(f32[3,128,8,128]{3,2,1,0:T(8,128)S(1)} %get-tuple-element.15.local_ref, f32[16,3,8,128]{3,2,1,0:T(8,128)S(1)} %bitcast.23, f32[3,8,8,128]{3,2,1,0:T(8,128)S(1)} %get-tuple-element.17.start_ref, f32[2,8,8,128]{3,2,1,0:T(8,128)S(1)} %get-tuple-element.18.chunk_ref, ...), custom_call_target="tpu_custom_call" | custom-call | tf_op jit(solution)/shard_map/pallas_call | solution.py:317
  (1 shorter events, 0.0 us)
Async XLA Ops:
  13.7 6.0 %collective-permute-start.3 = (f32[24,128]{1,0:T(8,128)S(1)}, f32[24,128]{1,0:T(8,128)S(1)}, u32[]{:S(2)}, u32[]{:S(2)}) collective-permute-start(f32[24,128]{1,0:T(8,128)S(1)} %bitcast.25), channel_id=1, source_target_pairs={{0,16},{1,17},{2,18},{3,19},{4,20},{5,21},{6,22},{7,23},{8,24},{9,... | collective-permute-start | bytes 36872 | tf_op jit(solution)/shard_map/ppermute | solution.py:316
  14.4 5.3 %collective-permute-start.2 = (f32[24,128]{1,0:T(8,128)S(1)}, f32[24,128]{1,0:T(8,128)S(1)}, u32[]{:S(2)}, u32[]{:S(2)}) collective-permute-start(f32[24,128]{1,0:T(8,128)S(1)} %bitcast.26), channel_id=1, source_target_pairs={{0,48},{1,49},{2,50},{3,51},{4,52},{5,53},{6,54},{7,55},{8,56},{9,... | collective-permute-start | bytes 36872 | tf_op jit(solution)/shard_map/ppermute | solution.py:316
  15.0 8.6 %collective-permute-start.1 = (f32[24,128]{1,0:T(8,128)S(1)}, f32[24,128]{1,0:T(8,128)S(1)}, u32[]{:S(2)}, u32[]{:S(2)}) collective-permute-start(f32[24,128]{1,0:T(8,128)S(1)} %bitcast.27), channel_id=1, source_target_pairs={{0,40},{1,41},{2,42},{3,43},{4,44},{5,45},{6,46},{7,47},{8,32},{9,... | collective-permute-start | bytes 36872 | tf_op jit(solution)/shard_map/ppermute | solution.py:316
  16.3 8.5 %collective-permute-start = (f32[24,128]{1,0:T(8,128)S(1)}, f32[24,128]{1,0:T(8,128)S(1)}, u32[]{:S(2)}, u32[]{:S(2)}) collective-permute-start(f32[24,128]{1,0:T(8,128)S(1)} %bitcast.28), channel_id=1, source_target_pairs={{16,32},{17,33},{18,34},{19,35},{20,36},{21,37},{22,38},{23,39},{2... | collective-permute-start | bytes 36872 | tf_op jit(solution)/shard_map/ppermute | solution.py:316

commit v4 on v3

v4 whole, which is shorter than its diff:
```python
import functools

import jax
import jax.numpy as jnp
from jax import lax
from jax.experimental import pallas as pl
from jax.experimental.pallas import tpu as pltpu
from jax.sharding import Mesh
from jax.sharding import PartitionSpec as P

LANES = 128
ROWS = 8
STEP = 16
NEAR = 16
FAR = 4
WIDE = 8
SENDS = (
    ((0, 1, 0),),
    ((0, 3, 0),),
    ((0, 2, 1), (1, 3, 1)),
    ((1, 2, 0), (2, 3, 0)),
)

HBM = pl.BlockSpec(memory_space=pltpu.HBM)
VMEM = pl.BlockSpec(memory_space=pltpu.VMEM)
LIMIT = pltpu.CompilerParams(vmem_limit_bytes=8 * 1024 * 1024)


def times(one, two):
    a, b = one
    c, d = two
    return (a * c - b * d, a * d + b * c)


def powers(base, count):
    found = [None, base]
    for n in range(2, count):
        found.append(times(found[n // 2], found[n - n // 2]))
    return found


def places():
    return lax.broadcasted_iota(jnp.int32, (ROWS, LANES), 0)


def sign():
    return jnp.where(places() % 2 == 0, -1.0, 1.0)


def swapped(value):
    return jnp.take_along_axis(value, places() ^ 1, axis=0, mode="promise_in_bounds")


def spread(row):
    return jnp.broadcast_to(row, (ROWS, LANES))


def doubled(rows):
    return jnp.concatenate([rows[j // 2 : j // 2 + 1] for j in range(ROWS)], axis=0)


TURNS = ((1, 4), (4, 4), (16, 4), (64, 2))


def turned_product(value, width, turns):
    rolled = [value] + [pltpu.roll(value, width * n, 1) for n in range(1, turns)]
    while len(rolled) > 1:
        rolled = [rolled[n] * rolled[n + 1] for n in range(0, len(rolled), 2)]
    return rolled[0]


def lane_product(value):
    for width, turns in TURNS:
        value = turned_product(value, width, turns)
    return value


def windows(value):
    for width, turns in TURNS[:2]:
        value = turned_product(value, width, turns)
    return value


def minus_expm1_twice(rate):
    u = 2.0 * rate
    series = u * (1.0 - u / 2 * (1.0 - u / 3 * (1.0 - u / 4 * (1.0 - u / 5 * (1.0 - u / 6)))))
    return jnp.where(u < 0.1, series, 1.0 - jnp.exp(-u))


def first(batch, length, x_hbm, rate_hbm, phase_hbm, keep_hbm, x_ref, send_ref, ends_ref, step_ref, chunk_ref, block_ref,
          small_ref, ended_ref, kept_ref, total_ref, near_ref, keep_ref, param_ref, own_ref, sems):
    me = lax.axis_index("seq")
    run = me // NEAR
    chunks = length // STEP
    span = length * ROWS
    pieces = [
        pltpu.make_async_copy(x_hbm.at[pl.ds(s * span, span)], x_ref.at[pl.ds(s * span, span)], sems.at[4 + s])
        for s in range(batch)
    ]
    loads = [
        pltpu.make_async_copy(rate_hbm, param_ref.at[0], sems.at[0]),
        pltpu.make_async_copy(phase_hbm, param_ref.at[1], sems.at[1]),
        pltpu.make_async_copy(keep_hbm.at[me], own_ref.at[pl.ds(0, batch)], sems.at[2]),
        pltpu.make_async_copy(keep_hbm, keep_ref, sems.at[3]),
    ]
    own_ref[...] = jnp.ones_like(own_ref)
    for load in loads[:3] + pieces[:1] + loads[3:] + pieces[1:]:
        load.start()
    flip = sign()
    loads[0].wait()
    loads[1].wait()
    loads[2].wait()
    own = own_ref[...]
    upright = jnp.transpose(own)
    for s in range(batch):
        for t in range(0, length, ROWS):
            kept_ref[s, pl.ds(t, ROWS)] = jnp.broadcast_to(upright[t : t + ROWS, s : s + 1], (ROWS, LANES))
    ended = windows(own)
    rate, phase = doubled(param_ref[0]), doubled(param_ref[1])
    magnitude = jnp.exp(-rate)
    one, zero = jnp.ones_like(rate), jnp.zeros_like(rate)
    lam = (magnitude * jnp.cos(phase), magnitude * jnp.sin(phase))
    gamma = jnp.sqrt(minus_expm1_twice(rate))
    step = powers(lam, STEP + 1)
    chunk = powers(step[STEP], chunks + 1)
    block = powers(chunk[chunks], NEAR + 1)
    small_ref[0] = gamma
    for part in range(2):
        small_ref[1 + part] = block[NEAR][part]
        for n in range(STEP):
            step_ref[part, n] = step[n + 1][part]
        chunk_ref[part, 0] = zero if part else one
        for n in range(1, chunks):
            chunk_ref[part, n] = chunk[n][part]
        for n in range(NEAR):
            block_ref[part, n] = zero
        block_ref[part, NEAR] = zero if part else one
        for n in range(1, NEAR):
            block_ref[part, NEAR + n] = block[n][part]

    def ends(s):
        direct, cross = [None] * chunks, [None] * chunks
        for i in range(STEP):
            n = STEP - 1 - i
            for k in range(chunks):
                t = k * STEP + i
                x = x_ref[pl.ds(s * span + t * ROWS, ROWS)].astype(jnp.float32)
                if i == 0:
                    direct[k], cross[k] = step[n][0] * x, step[n][1] * x
                    continue
                kept = spread(kept_ref[s, pl.ds(t, 1)])
                direct[k] = kept * direct[k] + (step[n][0] * x if n else x)
                cross[k] = kept * cross[k] + step[n][1] * x if n else kept * cross[k]
        one_way = other = None
        for k in range(chunks):
            ends_ref[s, k, 0], ends_ref[s, k, 1] = direct[k], cross[k]
            last = k * STEP + STEP - 1
            decay = jnp.broadcast_to(ended[s : s + 1, last : last + 1], (ROWS, LANES))
            ended_ref[pl.ds(s * chunks + k, 1)] = decay[:1]
            if k < chunks - 1:
                n = chunks - 1 - k
                real = chunk[n][0] * direct[k] - chunk[n][1] * cross[k]
                imag = chunk[n][0] * cross[k] + chunk[n][1] * direct[k]
            else:
                real, imag = direct[k], cross[k]
            one_way, other = (real, imag) if k == 0 else (decay * one_way + real, decay * other + imag)
        state = gamma * (one_way + flip * swapped(other))
        for n in range(NEAR):
            send_ref[n, s] = state

    def weights(near):
        after = jnp.ones((batch, LANES), jnp.float32)
        for m in reversed(range(NEAR)):
            near_ref[m] = near[m]
            for s in range(batch):
                factor = spread(after[s : s + 1])
                for part in range(2):
                    total_ref[part, m, s] = factor * block_ref[part, 2 * NEAR - 1 - m]
            after = after * near[m]

    pieces[0].wait()
    ends(0)
    loads[3].wait()
    pieces[1].wait()
    near = [keep_ref[run * NEAR + m] for m in range(NEAR)]
    for width, turns in TURNS[:2]:
        near = [turned_product(value, width, turns) for value in near]
    ends(1)
    pieces[2].wait()
    for width, turns in TURNS[2:]:
        near = [turned_product(value, width, turns) for value in near]
    weights(near)
    ends(2)


def gathered(terms, flip):
    direct = cross = None
    for real, imag, x in terms:
        one, two = real * x, imag * x
        direct, cross = (one, two) if direct is None else (direct + one, cross + two)
    return direct + flip * swapped(cross)


def second(batch, got_ref, total_ref, send_ref):
    flip = sign()
    for s in range(batch):
        send_ref[s] = gathered([(total_ref[0, m, s], total_ref[1, m, s], got_ref[m, s]) for m in range(NEAR)], flip)


def middle(batch, length, x_ref, got_ref, ends_ref, step_ref, chunk_ref, block_ref, small_ref, ended_ref, kept_ref,
           near_ref, keep_ref, local_ref, decay_ref, inside_ref, lines_ref):
    me = lax.axis_index("seq")
    run, at = me // NEAR, me % NEAR
    chunks = length // STEP
    span = length * ROWS
    flip = sign()
    products = []
    for n in range(FAR):
        product = keep_ref[n * NEAR]
        for m in range(1, NEAR):
            product = product * keep_ref[n * NEAR + m]
        products.append(product)
    back = []
    for d in range(1, FAR - 1):
        before = products[0]
        for m in range(1, FAR):
            before = jnp.where(run - d == m, products[m], before)
        back.append(lane_product(before))

    gamma = small_ref[0]
    lam_re, lam_im = step_ref[0, 0], step_ref[1, 0] * flip
    jump_re, jump_im = step_ref[0, STEP - 1], step_ref[1, STEP - 1] * flip
    state, reach = {}, {}
    for s in range(batch):
        for k in range(chunks):
            if k == 0:
                state[s, k], reach[s, k] = jnp.zeros_like(gamma), jnp.ones_like(gamma)
                continue
            h = state[s, k - 1]
            decay = spread(ended_ref[pl.ds(s * chunks + k - 1, 1)])
            end = gamma * (ends_ref[s, k - 1, 0] + flip * swapped(ends_ref[s, k - 1, 1]))
            state[s, k] = decay * (jump_re * h + jump_im * swapped(h)) + end
            reach[s, k] = decay * reach[s, k - 1]
    for k in range(chunks):
        for i in range(STEP):
            t = k * STEP + i
            power = times((step_ref[0, i], step_ref[1, i]), (chunk_ref[0, k], chunk_ref[1, k]))
            for s in range(batch):
                kept = spread(kept_ref[s, pl.ds(t, 1)])
                x = gamma * x_ref[pl.ds(s * span + t * ROWS, ROWS)].astype(jnp.float32)
                h = state[s, k]
                state[s, k] = kept * (lam_re * h + lam_im * swapped(h)) + x
                reach[s, k] = kept * reach[s, k]
                local_ref[s, t] = state[s, k]
                for part in range(2):
                    decay_ref[part, s, t] = reach[s, k] * power[part]

    after = jnp.ones((batch, LANES), jnp.float32)
    terms = [[] for _ in range(batch)]
    for m in reversed(range(NEAR)):
        real, imag = block_ref[0, NEAR - 1 + at - m], block_ref[1, NEAR - 1 + at - m]
        for s in range(batch):
            factor = spread(after[s : s + 1])
            terms[s].append((factor * real, factor * imag, got_ref[m, s]))
        after = after * jnp.where(m < at, near_ref[m], 1.0)
    for s in range(batch):
        inside_ref[s] = gathered(terms[s], flip)
    weight = (block_ref[0, NEAR + at], block_ref[1, NEAR + at])
    for d in range(1, FAR):
        for s in range(batch):
            factor = spread(after[s : s + 1])
            for part in range(2):
                lines_ref[part, d - 1, s] = factor * weight[part]
        if d < FAR - 1:
            after = after * back[d - 1]
            weight = times(weight, (small_ref[1], small_ref[2]))


def third(batch, length, local_ref, decay_ref, inside_ref, lines_ref, *rest):
    far_refs, (y_hbm, y_ref, sems) = rest[: len(SENDS)], rest[len(SENDS) :]
    run = lax.axis_index("seq") // NEAR
    flip = sign()
    size = length // 2
    stores = []
    for s in range(batch):
        terms = []
        for sends, far_ref in zip(SENDS, reversed(far_refs)):
            d = sum(jnp.where(run == to, to - at - 1, 0) for at, to, _ in sends)
            terms.append((lines_ref[0, d, s], lines_ref[1, d, s], far_ref[s]))
        carry = inside_ref[s] + gathered(terms, flip)
        turned = flip * swapped(carry)
        for half in range(2):
            for t in range(half * size, half * size + size):
                state = local_ref[s, t] + (decay_ref[0, s, t] * carry + decay_ref[1, s, t] * turned)
                y_ref[pl.ds((s * length + t) * ROWS, ROWS)] = state.astype(jnp.bfloat16)
            rows = pl.ds((2 * s + half) * size * ROWS, size * ROWS)
            store = pltpu.make_async_copy(y_ref.at[rows], y_hbm.at[rows], sems.at[2 * s + half])
            store.start()
            stores.append(store)
    for store in stores:
        store.wait()


def shards(inputs, decay_rate, phase, keep):
    batch, length, parts, width = inputs.shape
    tiles = width // LANES
    blocks = keep.shape[1] // length
    chunks = length // STEP
    f32 = functools.partial(jax.ShapeDtypeStruct, dtype=jnp.float32)
    tile = (ROWS, LANES)
    total = batch * length * ROWS
    x = inputs.reshape(batch, length, parts, tiles, LANES).transpose(0, 1, 3, 2, 4).reshape(total, LANES)
    kept = keep.reshape(batch, blocks, length).transpose(1, 0, 2)
    given = (x, decay_rate.reshape(tiles, LANES), phase.reshape(tiles, LANES), kept)
    x, send, ends, step, chunk, block, small, ended, kepts, totals, products, keeps = pl.pallas_call(
        functools.partial(first, batch, length),
        out_shape=[
            jax.ShapeDtypeStruct((total, LANES), jnp.bfloat16),
            f32((NEAR, batch, *tile)),
            f32((batch, chunks, 2, *tile)),
            f32((2, STEP, *tile)),
            f32((2, chunks, *tile)),
            f32((2, 2 * NEAR, *tile)),
            f32((3, *tile)),
            f32((batch * chunks, LANES)),
            f32((batch, length, LANES)),
            f32((2, NEAR, batch, *tile)),
            f32((NEAR, batch, LANES)),
            f32((blocks, batch, LANES)),
        ],
        in_specs=[HBM] * 4,
        out_specs=[VMEM] * 12,
        scratch_shapes=[
            pltpu.VMEM((2, tiles, LANES), jnp.float32),
            pltpu.VMEM((ROWS, LANES), jnp.float32),
            pltpu.SemaphoreType.DMA((4 + batch,)),
        ],
        compiler_params=LIMIT,
    )(*(pltpu.with_memory_space_constraint(value, pltpu.HBM) for value in given))

    runs = range(blocks // NEAR)
    near = lax.all_to_all(
        send.reshape(NEAR, batch * ROWS, LANES),
        "seq",
        0,
        0,
        axis_index_groups=[[run * NEAR + m for m in range(NEAR)] for run in runs],
        tiled=True,
    ).reshape(send.shape)
    sums = pl.pallas_call(
        functools.partial(second, batch),
        out_shape=f32((batch, *tile)),
        in_specs=[VMEM] * 2,
        out_specs=VMEM,
        compiler_params=LIMIT,
    )(near, totals)
    flat = sums.reshape(batch * ROWS, LANES)
    far = []
    for sends in SENDS:
        pairs = [
            (at * NEAR + m, to * NEAR + (m + cross * WIDE) % NEAR) for at, to, cross in sends for m in range(NEAR)
        ]
        far.append(lax.ppermute(flat, "seq", pairs).reshape(sums.shape))
    local, decay, inside, lines = pl.pallas_call(
        functools.partial(middle, batch, length),
        out_shape=[
            f32((batch, length, *tile)),
            f32((2, batch, length, *tile)),
            f32((batch, *tile)),
            f32((2, FAR - 1, batch, *tile)),
        ],
        in_specs=[VMEM] * 11,
        out_specs=[VMEM] * 4,
        compiler_params=LIMIT,
        cost_estimate=pl.CostEstimate(flops=10_000_000, bytes_accessed=6_000_000, transcendentals=0),
    )(x, near, ends, step, chunk, block, small, ended, kepts, products, keeps)
    y = pl.pallas_call(
        functools.partial(third, batch, length),
        out_shape=jax.ShapeDtypeStruct((total, LANES), jnp.bfloat16),
        in_specs=[VMEM] * (4 + len(SENDS)),
        out_specs=HBM,
        scratch_shapes=[
            pltpu.VMEM((total, LANES), jnp.bfloat16),
            pltpu.SemaphoreType.DMA((2 * batch,)),
        ],
        compiler_params=LIMIT,
    )(local, decay, inside, lines, *reversed(far))
    y = y.reshape(batch, length, tiles, parts, LANES).transpose(0, 1, 3, 2, 4)
    return y.reshape(inputs.shape)


def solution(mesh):
    split = Mesh(mesh.devices, ("chan", "seq"))
    return jax.shard_map(
        shards,
        mesh=split,
        in_specs=(P(None, "seq", None, "chan"), P("chan"), P("chan"), P()),
        out_specs=P(None, "seq", None, "chan"),
        check_vma=False,
    )
```

time: 26.2 us -> 25.8 us (0.985)
  waiting for transfers between devices: 5.12 us -> 4.18 us
  Pallas kernels: 3.23 us -> 3.71 us
    ppermute x4, waiting for transfers between devices: 5.12 us -> 4.18 us  [shards(): far.append(lax.ppermute(flat, 'seq', pairs).reshape(sums.shape))]
    pallas_call x1 -> x2, Pallas kernels: 1.99 us -> 2.56 us  [the longest x1 1.63 us: shards(): pl.pallas_call(functools.partial(first, batch, length), out_shape=[jax.Sh...]
  transfers between devices with their start and end apart: 4 -> 4, of which waited for: 2 -> 2; matrix products, arithmetic and copies ran while one was open for 0% -> 0% of each run, Pallas kernels for 0% -> 4%
where the time goes in v4:
time: 25.8 us; the launch traced here: 25.5 us
  blocking collectives  11.6 us (45%)
  starting transfers between devices  5.94 us (23%)
  waiting for transfers between devices  4.18 us (16%)
  Pallas kernels  3.71 us (14%)
    all_to_all x1, blocking collectives, shards(): lax.all_to_all(send.reshape(NEAR, batch * ROWS, LANES), 'seq', 0, 0, axis...  11.6 us
    ppermute x4, starting transfers between devices, shards(): far.append(lax.ppermute(flat, 'seq', pairs).reshape(sums.shape))  5.94 us
    ppermute x4, waiting for transfers between devices, shards(): far.append(lax.ppermute(flat, 'seq', pairs).reshape(sums.shape))  4.18 us
    pallas_call x1, Pallas kernels, shards(): pl.pallas_call(functools.partial(first, batch, length), out_shape=[jax.Sh...  1.63 us
    pallas_call x1, Pallas kernels, shards(): pl.pallas_call(functools.partial(third, batch, length), out_shape=jax.Sha...  1.11 us
    pallas_call x1, Pallas kernels, shards(): pl.pallas_call(functools.partial(middle, batch, length), out_shape=[f32((...  0.93 us
  transfers between devices with their start and end apart: 4, of which 2 were waited for; matrix products, arithmetic and copies ran while one was open for 0% of the time, Pallas kernels for 4%

profile of v4, /device:TPU:488, one launch (start us, length us, event | category | flops | bytes accessed | tf_op | source)
XLA Modules:
  0.0 25.5 jit_solution(14846248500397991951)
XLA Ops:
  0.0 1.6 %shard_map.46 = (bf16[3072,128]{1,0:T(8,128)(2,1)S(1)}, f32[16,3,8,128]{3,2,1,0:T(8,128)S(1)}, f32[3,8,2,8,128]{4,3,2,1,0:T(8,128)S(1)}, f32[2,16,8,128]{3,2,1,0...) custom-call(bf16[3072,128]{1,0:T(8,128)(2,1)} %bitcast.33, ...), custom_call_target="tpu_custom_call" | custom-call | tf_op jit(solution)/shard_map/pallas_call | solution.py:315
  1.6 11.6 %all_to_all.5 = f32[16,24,128]{2,1,0:T(8,128)S(1)} all-to-all(f32[16,24,128]{2,1,0:T(8,128)S(1)} %bitcast.24), channel_id=1, replica_groups={{0,1,2,3,4,5,6,7,8,9,10,11,12,13,14,15},{16,17,18,19,20,21,22,23,24,25,..., dimensions={0} | all-to-all | bytes 393216 | tf_op jit(solution)/shard_map/all_to_all | solution.py:342
  13.3 0.7 %collective-permute-start.3 = (f32[24,128]{1,0:T(8,128)S(1)}, f32[24,128]{1,0:T(8,128)S(1)}, u32[]{:S(2)}, u32[]{:S(2)}) collective-permute-start(f32[24,128]{1,0:T(8,128)S(1)} %bitcast.29), channel_id=1, source_target_pairs={{0,16},{1,17},{2,18},{3,19},{4,20},{5,21},{6,22},{7,23},{8,24},{9,... | collective-permute-start | bytes 36872 | tf_op jit(solution)/shard_map/ppermute | solution.py:363
  14.0 0.7 %collective-permute-start.2 = (f32[24,128]{1,0:T(8,128)S(1)}, f32[24,128]{1,0:T(8,128)S(1)}, u32[]{:S(2)}, u32[]{:S(2)}) collective-permute-start(f32[24,128]{1,0:T(8,128)S(1)} %bitcast.30), channel_id=1, source_target_pairs={{0,48},{1,49},{2,50},{3,51},{4,52},{5,53},{6,54},{7,55},{8,56},{9,... | collective-permute-start | bytes 36872 | tf_op jit(solution)/shard_map/ppermute | solution.py:363
  14.7 1.3 %collective-permute-start.1 = (f32[24,128]{1,0:T(8,128)S(1)}, f32[24,128]{1,0:T(8,128)S(1)}, u32[]{:S(2)}, u32[]{:S(2)}) collective-permute-start(f32[24,128]{1,0:T(8,128)S(1)} %bitcast.31), channel_id=1, source_target_pairs={{0,40},{1,41},{2,42},{3,43},{4,44},{5,45},{6,46},{7,47},{8,32},{9,... | collective-permute-start | bytes 36872 | tf_op jit(solution)/shard_map/ppermute | solution.py:363
  16.0 3.3 %collective-permute-start = (f32[24,128]{1,0:T(8,128)S(1)}, f32[24,128]{1,0:T(8,128)S(1)}, u32[]{:S(2)}, u32[]{:S(2)}) collective-permute-start(f32[24,128]{1,0:T(8,128)S(1)} %bitcast.32), channel_id=1, source_target_pairs={{16,32},{17,33},{18,34},{19,35},{20,36},{21,37},{22,38},{23,39},{2... | collective-permute-start | bytes 36872 | tf_op jit(solution)/shard_map/ppermute | solution.py:363
  19.3 0.9 %shard_map.47 = (f32[3,128,8,128]{3,2,1,0:T(8,128)S(1)}, f32[2,3,128,8,128]{4,3,2,1,0:T(8,128)S(1)}, f32[3,8,128]{2,1,0:T(8,128)S(1)}, f32[2,3,3,8,128]{4,3,2,1,0:T(8,128)S(1)}) custom-call(bf16[3072,128]{1,0:T(8,128)(2,1)S(1)} %get-tuple-element.21.x_ref, f32[16,3,8,128]{3,2,1,0:T(8,128)S(1)} %bitcast.23, ...), custom_call_target="tpu_custom_call" | custom-call | flops 10000000 | bytes 6000000 | tf_op jit(solution)/shard_map/pallas_call | solution.py:364
  20.2 0.0 collective-permute-done.3
  20.2 0.0 collective-permute-done.2
  20.3 3.0 %collective-permute-done.1 = f32[24,128]{1,0:T(8,128)S(1)} collective-permute-done((f32[24,128]{1,0:T(8,128)S(1)}, f32[24,128]{1,0:T(8,128)S(1)}, u32[]{:S(2)}, u32[]{:S(2)}) %collective-permute-start.1) | collective-permute-done | bytes 12320 | tf_op jit(solution)/shard_map/ppermute | solution.py:363
  23.3 1.2 %collective-permute-done = f32[24,128]{1,0:T(8,128)S(1)} collective-permute-done((f32[24,128]{1,0:T(8,128)S(1)}, f32[24,128]{1,0:T(8,128)S(1)}, u32[]{:S(2)}, u32[]{:S(2)}) %collective-permute-start) | collective-permute-done | bytes 12320 | tf_op jit(solution)/shard_map/ppermute | solution.py:363
  24.4 1.1 %shard_map.49 = bf16[3072,128]{1,0:T(8,128)(2,1)} custom-call(f32[3,128,8,128]{3,2,1,0:T(8,128)S(1)} %get-tuple-element.32.local_ref, f32[2,3,128,8,128]{4,3,2,1,0:T(8,128)S(1)} %get-tuple-element.33.decay_ref, f32[3,8,128]{2,1,0:T(8,128)S(1)} %get-tuple-element.34.inside_ref, f32[2,3,3,8,128]{4,3,2,1,0:T(8,128)S(1)} %get-tuple-element.35.lines_ref, ...), custom_call_target="tpu_custom_call" | custom-call | tf_op jit(solution)/shard_map/pallas_call | solution.py:377
  (1 shorter events, 0.0 us)
Async XLA Ops:
  13.3 6.9 %collective-permute-start.3 = (f32[24,128]{1,0:T(8,128)S(1)}, f32[24,128]{1,0:T(8,128)S(1)}, u32[]{:S(2)}, u32[]{:S(2)}) collective-permute-start(f32[24,128]{1,0:T(8,128)S(1)} %bitcast.29), channel_id=1, source_target_pairs={{0,16},{1,17},{2,18},{3,19},{4,20},{5,21},{6,22},{7,23},{8,24},{9,... | collective-permute-start | bytes 36872 | tf_op jit(solution)/shard_map/ppermute | solution.py:363
  14.0 6.3 %collective-permute-start.2 = (f32[24,128]{1,0:T(8,128)S(1)}, f32[24,128]{1,0:T(8,128)S(1)}, u32[]{:S(2)}, u32[]{:S(2)}) collective-permute-start(f32[24,128]{1,0:T(8,128)S(1)} %bitcast.30), channel_id=1, source_target_pairs={{0,48},{1,49},{2,50},{3,51},{4,52},{5,53},{6,54},{7,55},{8,56},{9,... | collective-permute-start | bytes 36872 | tf_op jit(solution)/shard_map/ppermute | solution.py:363
  14.7 8.6 %collective-permute-start.1 = (f32[24,128]{1,0:T(8,128)S(1)}, f32[24,128]{1,0:T(8,128)S(1)}, u32[]{:S(2)}, u32[]{:S(2)}) collective-permute-start(f32[24,128]{1,0:T(8,128)S(1)} %bitcast.31), channel_id=1, source_target_pairs={{0,40},{1,41},{2,42},{3,43},{4,44},{5,45},{6,46},{7,47},{8,32},{9,... | collective-permute-start | bytes 36872 | tf_op jit(solution)/shard_map/ppermute | solution.py:363
  16.0 8.5 %collective-permute-start = (f32[24,128]{1,0:T(8,128)S(1)}, f32[24,128]{1,0:T(8,128)S(1)}, u32[]{:S(2)}, u32[]{:S(2)}) collective-permute-start(f32[24,128]{1,0:T(8,128)S(1)} %bitcast.32), channel_id=1, source_target_pairs={{16,32},{17,33},{18,34},{19,35},{20,36},{21,37},{22,38},{23,39},{2... | collective-permute-start | bytes 36872 | tf_op jit(solution)/shard_map/ppermute | solution.py:363

commit v5 on v4

--- a/solution.py
+++ b/solution.py
@@ -358,7 +358,7 @@
     far = []
     for sends in SENDS:
         pairs = [
-            (at * NEAR + m, to * NEAR + (m + cross * WIDE) % NEAR) for at, to, cross in sends for m in range(NEAR)
+            (at * NEAR + m, to * NEAR + ((m + cross * WIDE) % NEAR ^ 1)) for at, to, cross in sends for m in range(NEAR)
         ]
         far.append(lax.ppermute(flat, "seq", pairs).reshape(sums.shape))
     local, decay, inside, lines = pl.pallas_call(

time: 25.8 us -> 25.7 us (level)
  the two profiles are of different devices: /device:TPU:488 before, /device:TPU:1 now
where the time goes in v5:
time: 25.7 us; the launch traced here: 25.5 us
  blocking collectives  16 us (62%)
  starting transfers between devices  5.71 us (22%)
  Pallas kernels  3.73 us (15%)
    all_to_all x1, blocking collectives, shards(): lax.all_to_all(send.reshape(NEAR, batch * ROWS, LANES), 'seq', 0, 0, axis...  16 us
    ppermute x4, starting transfers between devices, shards(): far.append(lax.ppermute(flat, 'seq', pairs).reshape(sums.shape))  5.71 us
    pallas_call x1, Pallas kernels, shards(): pl.pallas_call(functools.partial(first, batch, length), out_shape=[jax.Sh...  1.63 us
    pallas_call x1, Pallas kernels, shards(): pl.pallas_call(functools.partial(third, batch, length), out_shape=jax.Sha...  1.12 us
    pallas_call x1, Pallas kernels, shards(): pl.pallas_call(functools.partial(middle, batch, length), out_shape=[f32((...  0.93 us
  transfers between devices with their start and end apart: 4, of which 0 were waited for; matrix products, arithmetic and copies ran while one was open for 0% of the time, Pallas kernels for 4%

profile of v5, /device:TPU:1, one launch (start us, length us, event | category | flops | bytes accessed | tf_op | source)
XLA Modules:
  0.0 25.5 jit_solution(5664565913275064842)
XLA Ops:
  0.0 1.6 %shard_map.46 = (bf16[3072,128]{1,0:T(8,128)(2,1)S(1)}, f32[16,3,8,128]{3,2,1,0:T(8,128)S(1)}, f32[3,8,2,8,128]{4,3,2,1,0:T(8,128)S(1)}, f32[2,16,8,128]{3,2,1,0...) custom-call(bf16[3072,128]{1,0:T(8,128)(2,1)} %bitcast.33, ...), custom_call_target="tpu_custom_call" | custom-call | tf_op jit(solution)/shard_map/pallas_call | solution.py:315
  1.6 16.0 %all_to_all.5 = f32[16,24,128]{2,1,0:T(8,128)S(1)} all-to-all(f32[16,24,128]{2,1,0:T(8,128)S(1)} %bitcast.24), channel_id=1, replica_groups={{0,1,2,3,4,5,6,7,8,9,10,11,12,13,14,15},{16,17,18,19,20,21,22,23,24,25,..., dimensions={0} | all-to-all | bytes 393216 | tf_op jit(solution)/shard_map/all_to_all | solution.py:342
  17.6 2.2 %collective-permute-start.3 = (f32[24,128]{1,0:T(8,128)S(1)}, f32[24,128]{1,0:T(8,128)S(1)}, u32[]{:S(2)}, u32[]{:S(2)}) collective-permute-start(f32[24,128]{1,0:T(8,128)S(1)} %bitcast.29), channel_id=1, source_target_pairs={{0,17},{1,16},{2,19},{3,18},{4,21},{5,20},{6,23},{7,22},{8,25},{9,... | collective-permute-start | bytes 36872 | tf_op jit(solution)/shard_map/ppermute | solution.py:363
  19.8 1.4 %collective-permute-start.2 = (f32[24,128]{1,0:T(8,128)S(1)}, f32[24,128]{1,0:T(8,128)S(1)}, u32[]{:S(2)}, u32[]{:S(2)}) collective-permute-start(f32[24,128]{1,0:T(8,128)S(1)} %bitcast.30), channel_id=1, source_target_pairs={{0,49},{1,48},{2,51},{3,50},{4,53},{5,52},{6,55},{7,54},{8,57},{9,... | collective-permute-start | bytes 36872 | tf_op jit(solution)/shard_map/ppermute | solution.py:363
  21.3 1.4 %collective-permute-start.1 = (f32[24,128]{1,0:T(8,128)S(1)}, f32[24,128]{1,0:T(8,128)S(1)}, u32[]{:S(2)}, u32[]{:S(2)}) collective-permute-start(f32[24,128]{1,0:T(8,128)S(1)} %bitcast.31), channel_id=1, source_target_pairs={{0,41},{1,40},{2,43},{3,42},{4,45},{5,44},{6,47},{7,46},{8,33},{9,... | collective-permute-start | bytes 36872 | tf_op jit(solution)/shard_map/ppermute | solution.py:363
  22.7 0.7 %collective-permute-start = (f32[24,128]{1,0:T(8,128)S(1)}, f32[24,128]{1,0:T(8,128)S(1)}, u32[]{:S(2)}, u32[]{:S(2)}) collective-permute-start(f32[24,128]{1,0:T(8,128)S(1)} %bitcast.32), channel_id=1, source_target_pairs={{16,33},{17,32},{18,35},{19,34},{20,37},{21,36},{22,39},{23,38},{2... | collective-permute-start | bytes 36872 | tf_op jit(solution)/shard_map/ppermute | solution.py:363
  23.4 0.9 %shard_map.47 = (f32[3,128,8,128]{3,2,1,0:T(8,128)S(1)}, f32[2,3,128,8,128]{4,3,2,1,0:T(8,128)S(1)}, f32[3,8,128]{2,1,0:T(8,128)S(1)}, f32[2,3,3,8,128]{4,3,2,1,0:T(8,128)S(1)}) custom-call(bf16[3072,128]{1,0:T(8,128)(2,1)S(1)} %get-tuple-element.21.x_ref, f32[16,3,8,128]{3,2,1,0:T(8,128)S(1)} %bitcast.23, ...), custom_call_target="tpu_custom_call" | custom-call | flops 10000000 | bytes 6000000 | tf_op jit(solution)/shard_map/pallas_call | solution.py:364
  24.3 0.0 collective-permute-done.3
  24.3 0.0 collective-permute-done.2
  24.3 0.0 collective-permute-done.1
  24.4 0.0 collective-permute-done
  24.4 1.1 %shard_map.49 = bf16[3072,128]{1,0:T(8,128)(2,1)} custom-call(f32[3,128,8,128]{3,2,1,0:T(8,128)S(1)} %get-tuple-element.32.local_ref, f32[2,3,128,8,128]{4,3,2,1,0:T(8,128)S(1)} %get-tuple-element.33.decay_ref, f32[3,8,128]{2,1,0:T(8,128)S(1)} %get-tuple-element.34.inside_ref, f32[2,3,3,8,128]{4,3,2,1,0:T(8,128)S(1)} %get-tuple-element.35.lines_ref, ...), custom_call_target="tpu_custom_call" | custom-call | tf_op jit(solution)/shard_map/pallas_call | solution.py:377
  (1 shorter events, 0.0 us)
Async XLA Ops:
  17.6 6.7 %collective-permute-start.3 = (f32[24,128]{1,0:T(8,128)S(1)}, f32[24,128]{1,0:T(8,128)S(1)}, u32[]{:S(2)}, u32[]{:S(2)}) collective-permute-start(f32[24,128]{1,0:T(8,128)S(1)} %bitcast.29), channel_id=1, source_target_pairs={{0,17},{1,16},{2,19},{3,18},{4,21},{5,20},{6,23},{7,22},{8,25},{9,... | collective-permute-start | bytes 36872 | tf_op jit(solution)/shard_map/ppermute | solution.py:363
  19.8 4.5 %collective-permute-start.2 = (f32[24,128]{1,0:T(8,128)S(1)}, f32[24,128]{1,0:T(8,128)S(1)}, u32[]{:S(2)}, u32[]{:S(2)}) collective-permute-start(f32[24,128]{1,0:T(8,128)S(1)} %bitcast.30), channel_id=1, source_target_pairs={{0,49},{1,48},{2,51},{3,50},{4,53},{5,52},{6,55},{7,54},{8,57},{9,... | collective-permute-start | bytes 36872 | tf_op jit(solution)/shard_map/ppermute | solution.py:363
  21.3 3.1 %collective-permute-start.1 = (f32[24,128]{1,0:T(8,128)S(1)}, f32[24,128]{1,0:T(8,128)S(1)}, u32[]{:S(2)}, u32[]{:S(2)}) collective-permute-start(f32[24,128]{1,0:T(8,128)S(1)} %bitcast.31), channel_id=1, source_target_pairs={{0,41},{1,40},{2,43},{3,42},{4,45},{5,44},{6,47},{7,46},{8,33},{9,... | collective-permute-start | bytes 36872 | tf_op jit(solution)/shard_map/ppermute | solution.py:363
  22.7 1.6 %collective-permute-start = (f32[24,128]{1,0:T(8,128)S(1)}, f32[24,128]{1,0:T(8,128)S(1)}, u32[]{:S(2)}, u32[]{:S(2)}) collective-permute-start(f32[24,128]{1,0:T(8,128)S(1)} %bitcast.32), channel_id=1, source_target_pairs={{16,33},{17,32},{18,35},{19,34},{20,37},{21,36},{22,39},{23,38},{2... | collective-permute-start | bytes 36872 | tf_op jit(solution)/shard_map/ppermute | solution.py:363

commit v6 on v5

--- a/solution.py
+++ b/solution.py
@@ -16,9 +16,9 @@
 WIDE = 8
 SENDS = (
     ((0, 1, 0),),
-    ((0, 3, 0),),
+    ((0, 3, 1),),
     ((0, 2, 1), (1, 3, 1)),
-    ((1, 2, 0), (2, 3, 0)),
+    ((1, 2, 0), (2, 3, 1)),
 )
 
 HBM = pl.BlockSpec(memory_space=pltpu.HBM)

time: 25.7 us -> 25.7 us (level)
  no operation moved by 1% of the time
where the time goes in v6:
time: 25.7 us; the launch traced here: 25.5 us
  blocking collectives  16 us (62%)
  starting transfers between devices  5.71 us (22%)
  Pallas kernels  3.73 us (15%)
    all_to_all x1, blocking collectives, shards(): lax.all_to_all(send.reshape(NEAR, batch * ROWS, LANES), 'seq', 0, 0, axis...  16 us
    ppermute x4, starting transfers between devices, shards(): far.append(lax.ppermute(flat, 'seq', pairs).reshape(sums.shape))  5.71 us
    pallas_call x1, Pallas kernels, shards(): pl.pallas_call(functools.partial(first, batch, length), out_shape=[jax.Sh...  1.63 us
    pallas_call x1, Pallas kernels, shards(): pl.pallas_call(functools.partial(third, batch, length), out_shape=jax.Sha...  1.12 us
    pallas_call x1, Pallas kernels, shards(): pl.pallas_call(functools.partial(middle, batch, length), out_shape=[f32((...  0.93 us
  transfers between devices with their start and end apart: 4, of which 0 were waited for; matrix products, arithmetic and copies ran while one was open for 0% of the time, Pallas kernels for 4%

profile of v6, /device:TPU:1, one launch (start us, length us, event | category | flops | bytes accessed | tf_op | source)
XLA Modules:
  0.0 25.5 jit_solution(5525709676609405529)
XLA Ops:
  0.0 1.6 %shard_map.46 = (bf16[3072,128]{1,0:T(8,128)(2,1)S(1)}, f32[16,3,8,128]{3,2,1,0:T(8,128)S(1)}, f32[3,8,2,8,128]{4,3,2,1,0:T(8,128)S(1)}, f32[2,16,8,128]{3,2,1,0...) custom-call(bf16[3072,128]{1,0:T(8,128)(2,1)} %bitcast.33, ...), custom_call_target="tpu_custom_call" | custom-call | tf_op jit(solution)/shard_map/pallas_call | solution.py:315
  1.6 16.0 %all_to_all.5 = f32[16,24,128]{2,1,0:T(8,128)S(1)} all-to-all(f32[16,24,128]{2,1,0:T(8,128)S(1)} %bitcast.24), channel_id=1, replica_groups={{0,1,2,3,4,5,6,7,8,9,10,11,12,13,14,15},{16,17,18,19,20,21,22,23,24,25,..., dimensions={0} | all-to-all | bytes 393216 | tf_op jit(solution)/shard_map/all_to_all | solution.py:342
  17.6 2.2 %collective-permute-start.3 = (f32[24,128]{1,0:T(8,128)S(1)}, f32[24,128]{1,0:T(8,128)S(1)}, u32[]{:S(2)}, u32[]{:S(2)}) collective-permute-start(f32[24,128]{1,0:T(8,128)S(1)} %bitcast.29), channel_id=1, source_target_pairs={{0,17},{1,16},{2,19},{3,18},{4,21},{5,20},{6,23},{7,22},{8,25},{9,... | collective-permute-start | bytes 36872 | tf_op jit(solution)/shard_map/ppermute | solution.py:363
  19.8 1.3 %collective-permute-start.2 = (f32[24,128]{1,0:T(8,128)S(1)}, f32[24,128]{1,0:T(8,128)S(1)}, u32[]{:S(2)}, u32[]{:S(2)}) collective-permute-start(f32[24,128]{1,0:T(8,128)S(1)} %bitcast.30), channel_id=1, source_target_pairs={{0,57},{1,56},{2,59},{3,58},{4,61},{5,60},{6,63},{7,62},{8,49},{9,... | collective-permute-start | bytes 36872 | tf_op jit(solution)/shard_map/ppermute | solution.py:363
  21.1 1.6 %collective-permute-start.1 = (f32[24,128]{1,0:T(8,128)S(1)}, f32[24,128]{1,0:T(8,128)S(1)}, u32[]{:S(2)}, u32[]{:S(2)}) collective-permute-start(f32[24,128]{1,0:T(8,128)S(1)} %bitcast.31), channel_id=1, source_target_pairs={{0,41},{1,40},{2,43},{3,42},{4,45},{5,44},{6,47},{7,46},{8,33},{9,... | collective-permute-start | bytes 36872 | tf_op jit(solution)/shard_map/ppermute | solution.py:363
  22.7 0.7 %collective-permute-start = (f32[24,128]{1,0:T(8,128)S(1)}, f32[24,128]{1,0:T(8,128)S(1)}, u32[]{:S(2)}, u32[]{:S(2)}) collective-permute-start(f32[24,128]{1,0:T(8,128)S(1)} %bitcast.32), channel_id=1, source_target_pairs={{16,33},{17,32},{18,35},{19,34},{20,37},{21,36},{22,39},{23,38},{2... | collective-permute-start | bytes 36872 | tf_op jit(solution)/shard_map/ppermute | solution.py:363
  23.4 0.9 %shard_map.47 = (f32[3,128,8,128]{3,2,1,0:T(8,128)S(1)}, f32[2,3,128,8,128]{4,3,2,1,0:T(8,128)S(1)}, f32[3,8,128]{2,1,0:T(8,128)S(1)}, f32[2,3,3,8,128]{4,3,2,1,0:T(8,128)S(1)}) custom-call(bf16[3072,128]{1,0:T(8,128)(2,1)S(1)} %get-tuple-element.21.x_ref, f32[16,3,8,128]{3,2,1,0:T(8,128)S(1)} %bitcast.23, ...), custom_call_target="tpu_custom_call" | custom-call | flops 10000000 | bytes 6000000 | tf_op jit(solution)/shard_map/pallas_call | solution.py:364
  24.3 0.0 collective-permute-done.3
  24.3 0.0 collective-permute-done.2
  24.3 0.0 collective-permute-done.1
  24.4 0.0 collective-permute-done
  24.4 1.1 %shard_map.49 = bf16[3072,128]{1,0:T(8,128)(2,1)} custom-call(f32[3,128,8,128]{3,2,1,0:T(8,128)S(1)} %get-tuple-element.32.local_ref, f32[2,3,128,8,128]{4,3,2,1,0:T(8,128)S(1)} %get-tuple-element.33.decay_ref, f32[3,8,128]{2,1,0:T(8,128)S(1)} %get-tuple-element.34.inside_ref, f32[2,3,3,8,128]{4,3,2,1,0:T(8,128)S(1)} %get-tuple-element.35.lines_ref, ...), custom_call_target="tpu_custom_call" | custom-call | tf_op jit(solution)/shard_map/pallas_call | solution.py:377
  (1 shorter events, 0.0 us)
Async XLA Ops:
  17.6 6.7 %collective-permute-start.3 = (f32[24,128]{1,0:T(8,128)S(1)}, f32[24,128]{1,0:T(8,128)S(1)}, u32[]{:S(2)}, u32[]{:S(2)}) collective-permute-start(f32[24,128]{1,0:T(8,128)S(1)} %bitcast.29), channel_id=1, source_target_pairs={{0,17},{1,16},{2,19},{3,18},{4,21},{5,20},{6,23},{7,22},{8,25},{9,... | collective-permute-start | bytes 36872 | tf_op jit(solution)/shard_map/ppermute | solution.py:363
  19.8 4.5 %collective-permute-start.2 = (f32[24,128]{1,0:T(8,128)S(1)}, f32[24,128]{1,0:T(8,128)S(1)}, u32[]{:S(2)}, u32[]{:S(2)}) collective-permute-start(f32[24,128]{1,0:T(8,128)S(1)} %bitcast.30), channel_id=1, source_target_pairs={{0,57},{1,56},{2,59},{3,58},{4,61},{5,60},{6,63},{7,62},{8,49},{9,... | collective-permute-start | bytes 36872 | tf_op jit(solution)/shard_map/ppermute | solution.py:363
  21.1 3.2 %collective-permute-start.1 = (f32[24,128]{1,0:T(8,128)S(1)}, f32[24,128]{1,0:T(8,128)S(1)}, u32[]{:S(2)}, u32[]{:S(2)}) collective-permute-start(f32[24,128]{1,0:T(8,128)S(1)} %bitcast.31), channel_id=1, source_target_pairs={{0,41},{1,40},{2,43},{3,42},{4,45},{5,44},{6,47},{7,46},{8,33},{9,... | collective-permute-start | bytes 36872 | tf_op jit(solution)/shard_map/ppermute | solution.py:363
  22.7 1.6 %collective-permute-start = (f32[24,128]{1,0:T(8,128)S(1)}, f32[24,128]{1,0:T(8,128)S(1)}, u32[]{:S(2)}, u32[]{:S(2)}) collective-permute-start(f32[24,128]{1,0:T(8,128)S(1)} %bitcast.32), channel_id=1, source_target_pairs={{16,33},{17,32},{18,35},{19,34},{20,37},{21,36},{22,39},{23,38},{2... | collective-permute-start | bytes 36872 | tf_op jit(solution)/shard_map/ppermute | solution.py:363

commit v7 on v5

--- a/solution.py
+++ b/solution.py
@@ -208,7 +208,7 @@
 
 
 def middle(batch, length, x_ref, got_ref, ends_ref, step_ref, chunk_ref, block_ref, small_ref, ended_ref, kept_ref,
-           near_ref, keep_ref, local_ref, decay_ref, inside_ref, lines_ref):
+           near_ref, keep_ref, local_ref, decay_ref, reach_ref, inside_ref, lines_ref):
     me = lax.axis_index("seq")
     run, at = me // NEAR, me % NEAR
     chunks = length // STEP
@@ -252,8 +252,9 @@
                 state[s, k] = kept * (lam_re * h + lam_im * swapped(h)) + x
                 reach[s, k] = kept * reach[s, k]
                 local_ref[s, t] = state[s, k]
-                for part in range(2):
-                    decay_ref[part, s, t] = reach[s, k] * power[part]
+                reach_ref[s, pl.ds(t, 1)] = reach[s, k][:1]
+            for part in range(2):
+                decay_ref[part, t] = power[part]
 
     after = jnp.ones((batch, LANES), jnp.float32)
     terms = [[] for _ in range(batch)]
@@ -276,7 +277,7 @@
             weight = times(weight, (small_ref[1], small_ref[2]))
 
 
-def third(batch, length, local_ref, decay_ref, inside_ref, lines_ref, *rest):
+def third(batch, length, local_ref, decay_ref, reach_ref, inside_ref, lines_ref, *rest):
     far_refs, (y_hbm, y_ref, sems) = rest[: len(SENDS)], rest[len(SENDS) :]
     run = lax.axis_index("seq") // NEAR
     flip = sign()
@@ -291,7 +292,8 @@
         turned = flip * swapped(carry)
         for half in range(2):
             for t in range(half * size, half * size + size):
-                state = local_ref[s, t] + (decay_ref[0, s, t] * carry + decay_ref[1, s, t] * turned)
+                kept = spread(reach_ref[s, pl.ds(t, 1)])
+                state = local_ref[s, t] + kept * (decay_ref[0, t] * carry + decay_ref[1, t] * turned)
                 y_ref[pl.ds((s * length + t) * ROWS, ROWS)] = state.astype(jnp.bfloat16)
             rows = pl.ds((2 * s + half) * size * ROWS, size * ROWS)
             store = pltpu.make_async_copy(y_ref.at[rows], y_hbm.at[rows], sems.at[2 * s + half])
@@ -361,30 +363,31 @@
             (at * NEAR + m, to * NEAR + ((m + cross * WIDE) % NEAR ^ 1)) for at, to, cross in sends for m in range(NEAR)
         ]
         far.append(lax.ppermute(flat, "seq", pairs).reshape(sums.shape))
-    local, decay, inside, lines = pl.pallas_call(
+    local, decay, reach, inside, lines = pl.pallas_call(
         functools.partial(middle, batch, length),
         out_shape=[
             f32((batch, length, *tile)),
-            f32((2, batch, length, *tile)),
+            f32((2, length, *tile)),
+            f32((batch, length, LANES)),
             f32((batch, *tile)),
             f32((2, FAR - 1, batch, *tile)),
         ],
         in_specs=[VMEM] * 11,
-        out_specs=[VMEM] * 4,
+        out_specs=[VMEM] * 5,
         compiler_params=LIMIT,
         cost_estimate=pl.CostEstimate(flops=10_000_000, bytes_accessed=6_000_000, transcendentals=0),
     )(x, near, ends, step, chunk, block, small, ended, kepts, products, keeps)
     y = pl.pallas_call(
         functools.partial(third, batch, length),
         out_shape=jax.ShapeDtypeStruct((total, LANES), jnp.bfloat16),
-        in_specs=[VMEM] * (4 + len(SENDS)),
+        in_specs=[VMEM] * (5 + len(SENDS)),
         out_specs=HBM,
         scratch_shapes=[
             pltpu.VMEM((total, LANES), jnp.bfloat16),
             pltpu.SemaphoreType.DMA((2 * batch,)),
         ],
         compiler_params=LIMIT,
-    )(local, decay, inside, lines, *reversed(far))
+    )(local, decay, reach, inside, lines, *reversed(far))
     y = y.reshape(batch, length, tiles, parts, LANES).transpose(0, 1, 3, 2, 4)
     return y.reshape(inputs.shape)
 

time: 25.7 us -> 25.7 us (level)
  transfers between devices with their start and end apart: 4 -> 4, of which waited for: 0 -> 0; matrix products, arithmetic and copies ran while one was open for 0% -> 0% of each run, Pallas kernels for 4% -> 3%
where the time goes in v7:
time: 25.7 us; the launch traced here: 25.5 us
  blocking collectives  16 us (62%)
  starting transfers between devices  5.71 us (22%)
  Pallas kernels  3.74 us (15%)
    all_to_all x1, blocking collectives, shards(): lax.all_to_all(send.reshape(NEAR, batch * ROWS, LANES), 'seq', 0, 0, axis...  16 us
    ppermute x4, starting transfers between devices, shards(): far.append(lax.ppermute(flat, 'seq', pairs).reshape(sums.shape))  5.71 us
    pallas_call x1, Pallas kernels, shards(): pl.pallas_call(functools.partial(first, batch, length), out_shape=[jax.Sh...  1.64 us
    pallas_call x1, Pallas kernels, shards(): pl.pallas_call(functools.partial(third, batch, length), out_shape=jax.Sha...  1.22 us
    pallas_call x1, Pallas kernels, shards(): pl.pallas_call(functools.partial(middle, batch, length), out_shape=[f32((...  0.84 us
  transfers between devices with their start and end apart: 4, of which 0 were waited for; matrix products, arithmetic and copies ran while one was open for 0% of the time, Pallas kernels for 3%

profile of v7, /device:TPU:1, one launch (start us, length us, event | category | flops | bytes accessed | tf_op | source)
XLA Modules:
  0.0 25.5 jit_solution(6731737080299477947)
XLA Ops:
  0.0 1.6 %shard_map.46 = (bf16[3072,128]{1,0:T(8,128)(2,1)S(1)}, f32[16,3,8,128]{3,2,1,0:T(8,128)S(1)}, f32[3,8,2,8,128]{4,3,2,1,0:T(8,128)S(1)}, f32[2,16,8,128]{3,2,1,0...) custom-call(bf16[3072,128]{1,0:T(8,128)(2,1)} %bitcast.33, ...), custom_call_target="tpu_custom_call" | custom-call | tf_op jit(solution)/shard_map/pallas_call | solution.py:317
  1.6 16.0 %all_to_all.5 = f32[16,24,128]{2,1,0:T(8,128)S(1)} all-to-all(f32[16,24,128]{2,1,0:T(8,128)S(1)} %bitcast.24), channel_id=1, replica_groups={{0,1,2,3,4,5,6,7,8,9,10,11,12,13,14,15},{16,17,18,19,20,21,22,23,24,25,..., dimensions={0} | all-to-all | bytes 393216 | tf_op jit(solution)/shard_map/all_to_all | solution.py:344
  17.7 2.2 %collective-permute-start.3 = (f32[24,128]{1,0:T(8,128)S(1)}, f32[24,128]{1,0:T(8,128)S(1)}, u32[]{:S(2)}, u32[]{:S(2)}) collective-permute-start(f32[24,128]{1,0:T(8,128)S(1)} %bitcast.25), channel_id=1, source_target_pairs={{0,17},{1,16},{2,19},{3,18},{4,21},{5,20},{6,23},{7,22},{8,25},{9,... | collective-permute-start | bytes 36872 | tf_op jit(solution)/shard_map/ppermute | solution.py:365
  19.9 1.4 %collective-permute-start.2 = (f32[24,128]{1,0:T(8,128)S(1)}, f32[24,128]{1,0:T(8,128)S(1)}, u32[]{:S(2)}, u32[]{:S(2)}) collective-permute-start(f32[24,128]{1,0:T(8,128)S(1)} %bitcast.26), channel_id=1, source_target_pairs={{0,49},{1,48},{2,51},{3,50},{4,53},{5,52},{6,55},{7,54},{8,57},{9,... | collective-permute-start | bytes 36872 | tf_op jit(solution)/shard_map/ppermute | solution.py:365
  21.3 1.4 %collective-permute-start.1 = (f32[24,128]{1,0:T(8,128)S(1)}, f32[24,128]{1,0:T(8,128)S(1)}, u32[]{:S(2)}, u32[]{:S(2)}) collective-permute-start(f32[24,128]{1,0:T(8,128)S(1)} %bitcast.27), channel_id=1, source_target_pairs={{0,41},{1,40},{2,43},{3,42},{4,45},{5,44},{6,47},{7,46},{8,33},{9,... | collective-permute-start | bytes 36872 | tf_op jit(solution)/shard_map/ppermute | solution.py:365
  22.7 0.7 %collective-permute-start = (f32[24,128]{1,0:T(8,128)S(1)}, f32[24,128]{1,0:T(8,128)S(1)}, u32[]{:S(2)}, u32[]{:S(2)}) collective-permute-start(f32[24,128]{1,0:T(8,128)S(1)} %bitcast.28), channel_id=1, source_target_pairs={{16,33},{17,32},{18,35},{19,34},{20,37},{21,36},{22,39},{23,38},{2... | collective-permute-start | bytes 36872 | tf_op jit(solution)/shard_map/ppermute | solution.py:365
  23.4 0.8 %shard_map.47 = (f32[3,128,8,128]{3,2,1,0:T(8,128)S(1)}, f32[2,128,8,128]{3,2,1,0:T(8,128)S(1)}, f32[3,128,128]{2,1,0:T(8,128)S(1)}, f32[3,8,128]{2,1,0:T(8,128)S(1)}, f32[2,3,3,8,128]{4,3,2,1,0:T(8,128)S(1)}) custom-call(bf16[3072,128]{1,0:T(8,128)(2,1)S(1)} %get-tuple-element.22.x_ref, f32[16,3,8,128]{3,2,1,0:T(8,128)S(1)} %bitcast.23, ...), custom_call_target="tpu_custom_call" | custom-call | flops 10000000 | bytes 6000000 | tf_op jit(solution)/shard_map/pallas_call | solution.py:366
  24.2 0.0 collective-permute-done.3
  24.2 0.0 collective-permute-done.2
  24.3 0.0 collective-permute-done.1
  24.3 0.0 collective-permute-done
  24.3 1.2 %shard_map.49 = bf16[3072,128]{1,0:T(8,128)(2,1)} custom-call(f32[3,128,8,128]{3,2,1,0:T(8,128)S(1)} %get-tuple-element.33.local_ref, f32[2,128,8,128]{3,2,1,0:T(8,128)S(1)} %get-tuple-element.34.decay_ref, f32[3,128,128]{2,1,0:T(8,128)S(1)} %get-tuple-element.35.reach_ref, f32[3,8,128]{2,1,0:T(8,128)S(1)} %get-tuple-element.36.inside_ref, ...), custom_call_target="tpu_custom_call" | custom-call | tf_op jit(solution)/shard_map/pallas_call | solution.py:380
  (1 shorter events, 0.0 us)
Async XLA Ops:
  17.7 6.6 %collective-permute-start.3 = (f32[24,128]{1,0:T(8,128)S(1)}, f32[24,128]{1,0:T(8,128)S(1)}, u32[]{:S(2)}, u32[]{:S(2)}) collective-permute-start(f32[24,128]{1,0:T(8,128)S(1)} %bitcast.25), channel_id=1, source_target_pairs={{0,17},{1,16},{2,19},{3,18},{4,21},{5,20},{6,23},{7,22},{8,25},{9,... | collective-permute-start | bytes 36872 | tf_op jit(solution)/shard_map/ppermute | solution.py:365
  19.9 4.4 %collective-permute-start.2 = (f32[24,128]{1,0:T(8,128)S(1)}, f32[24,128]{1,0:T(8,128)S(1)}, u32[]{:S(2)}, u32[]{:S(2)}) collective-permute-start(f32[24,128]{1,0:T(8,128)S(1)} %bitcast.26), channel_id=1, source_target_pairs={{0,49},{1,48},{2,51},{3,50},{4,53},{5,52},{6,55},{7,54},{8,57},{9,... | collective-permute-start | bytes 36872 | tf_op jit(solution)/shard_map/ppermute | solution.py:365
  21.3 3.0 %collective-permute-start.1 = (f32[24,128]{1,0:T(8,128)S(1)}, f32[24,128]{1,0:T(8,128)S(1)}, u32[]{:S(2)}, u32[]{:S(2)}) collective-permute-start(f32[24,128]{1,0:T(8,128)S(1)} %bitcast.27), channel_id=1, source_target_pairs={{0,41},{1,40},{2,43},{3,42},{4,45},{5,44},{6,47},{7,46},{8,33},{9,... | collective-permute-start | bytes 36872 | tf_op jit(solution)/shard_map/ppermute | solution.py:365
  22.7 1.5 %collective-permute-start = (f32[24,128]{1,0:T(8,128)S(1)}, f32[24,128]{1,0:T(8,128)S(1)}, u32[]{:S(2)}, u32[]{:S(2)}) collective-permute-start(f32[24,128]{1,0:T(8,128)S(1)} %bitcast.28), channel_id=1, source_target_pairs={{16,33},{17,32},{18,35},{19,34},{20,37},{21,36},{22,39},{23,38},{2... | collective-permute-start | bytes 36872 | tf_op jit(solution)/shard_map/ppermute | solution.py:365
